TPU v7x, 32 devices: a whole 2x2x4 slice. The times are simulated.
32 devices in a mesh: row: 4 (over y, x), col: 8 (over z, core).
Axes of the slice: x: 2, y: 2, z: 4, core: 2. Of those that a mesh axis runs over, the one named last changes fastest.
Arguments:
- basis: bfloat16 [40, 131072], P(None, ('row', 'col'))
- expand: float32 [3, 8, 40], replicated, may hold values from -1 to 1
- tiles: bfloat16 [3, 3072, 128, 128], P(None, ('row', 'col')), may hold values from -0.3125 to 0.3125
- tile_rows: int32 [3072], P(('row', 'col')), may hold values from 0 to 255, as said below
- tile_cols: int32 [3072], P(('row', 'col')), may hold values from 0 to 127
Outputs:
- new_block: float32 [8, 131072], P(None, ('row', 'col'))
- coefficients: float32 [8, 40], replicated
- factor: float32 [8, 8], replicated
Inputs may be any that keep to these rules, and one draw needn't show every extreme that they name: `tile_rows`: each device's 96 tiles come in 8 runs of 12; the row tiles of run k are 12 distinct values from k * 32 to (k + 1) * 32 - 1.
All inputs are finite; a program needn't handle non-finite values.
Results may differ from a plain program's by a relative error of at most 0.0054.
Values may be sent and summed in bfloat16 or wider, within the bound.
A program may use at most 64 MiB of HBM per device.

v0:
```python
import functools
import math

import jax
import jax.numpy as jnp
from jax import lax
from jax.experimental import pallas as pl
from jax.experimental.pallas import tpu as pltpu
from jax.sharding import PartitionSpec as P

F32 = jnp.float32
BF16 = jnp.bfloat16
NT = (((1,), (1,)), ((), ()))


def exact(a, b, dims=(((1,), (0,)), ((), ()))):
    return lax.dot_general(a, b, dims, precision=lax.Precision.HIGHEST, preferred_element_type=F32)


def pieces(x):
    one = x.astype(BF16).astype(F32)
    rest = x - one
    two = rest.astype(BF16).astype(F32)
    three = rest - two
    return jnp.concatenate([one, two, three], axis=0).astype(BF16)


def fold(x, rows):
    return x[:rows] + x[rows : 2 * rows] + x[2 * rows :]


def kernel(
    nrow,
    ncol,
    expand_hbm,
    rows_hbm,
    picks_hbm,
    basis_hbm,
    tiles_hbm,
    new_ref,
    coef_ref,
    factor_ref,
    expand_ref,
    rows_ref,
    picks_ref,
    basis,
    tiles,
    cols,
    outbox,
    inbox,
    seg_out,
    seg_in,
    corr_col,
    corr_row,
    tail_col,
    tail_row,
    spread,
    app,
    small_sem,
    basis_sem,
    tile_sem,
    ser_send,
    ser_recv,
    fwd_send,
    fwd_recv,
    seg_send,
    seg_recv,
    box_send,
    box_recv,
    cc_send,
    cc_recv,
    cr_send,
    cr_recv,
    tc_send,
    tc_recv,
    tr_send,
    tr_recv,
):
    r = lax.axis_index("row")
    c = lax.axis_index("col")
    krylov, length = basis.shape
    kinds, tpd, tile, _ = tiles.shape
    cap = tpd // ncol
    region = length // tile
    bs = expand_ref.shape[1]
    entries = length * nrow * ncol
    inverse_root = 1.0 / math.sqrt(entries)
    width = seg_in.shape[2]

    load_basis = pltpu.make_async_copy(basis_hbm, basis, basis_sem)
    load_basis.start()
    small = [
        pltpu.make_async_copy(src, dst, small_sem.at[i])
        for i, (src, dst) in enumerate(((expand_hbm, expand_ref), (rows_hbm, rows_ref), (picks_hbm, picks_ref)))
    ]
    for copy in small:
        copy.start()

    def chunk_copy(m, k):
        part = pl.ds(k * cap, cap)
        return pltpu.make_async_copy(tiles_hbm.at[m, part], tiles.at[m, part], tile_sem.at[m, k])

    for j in range(1, ncol + 1):
        k = lax.rem(c + j, ncol)
        for m in range(kinds):
            chunk_copy(m, k).start()

    barrier = pltpu.get_barrier_semaphore()
    for j in range(1, nrow):
        pl.semaphore_signal(barrier, inc=1, device_id={"row": lax.rem(r + j, nrow)}, device_id_type=pl.DeviceIdType.MESH)
    for j in range(1, ncol):
        pl.semaphore_signal(barrier, inc=1, device_id={"col": lax.rem(c + j, ncol)}, device_id_type=pl.DeviceIdType.MESH)

    def remote(src, dst, send_sem, recv_sem, where):
        return pltpu.make_async_remote_copy(
            src_ref=src, dst_ref=dst, send_sem=send_sem, recv_sem=recv_sem,
            device_id=where, device_id_type=pl.DeviceIdType.MESH,
        )

    def row_at(j):
        peer = lax.rem(r + j, nrow)
        return peer, {"row": peer}

    def col_at(j):
        peer = lax.rem(c + j, ncol)
        return peer, {"col": peer}

    for copy in small:
        copy.wait()
    load_basis.wait()
    expand = pieces(expand_ref[...].reshape(kinds * bs, krylov))
    for l in range(region):
        part = fold(jnp.dot(expand, basis[:, l * tile : (l + 1) * tile], preferred_element_type=F32), kinds * bs)
        for m in range(kinds):
            cols[m, r * region + l] = part[m * bs : (m + 1) * bs].astype(BF16)

    pl.semaphore_wait(barrier, nrow + ncol - 2)

    outer = nrow // 2
    side, pair = lax.rem(r, 2), lax.div(r, 2)
    mate = r + 1 - 2 * side
    others = [2 * lax.rem(pair + j, outer) + side for j in range(1, outer)]
    half = region // 2

    def series_copy(m, owner, peer):
        block = cols.at[m, pl.ds(owner * region, region)]
        return remote(block, block, ser_send.at[m, peer], ser_recv.at[m, owner], {"row": peer})

    def pass_on(m, owner, h, peer, slot):
        block = cols.at[m, pl.ds(owner * region + h * half, half)]
        return remote(block, block, fwd_send.at[m, slot, h], fwd_recv.at[m, owner, h], {"row": peer})

    direct = [mate] + others
    for m in range(kinds):
        for peer in direct:
            series_copy(m, r, peer).start()

    slot = lax.broadcasted_iota(jnp.int32, (1, width), 1)
    for k in range(ncol):
        line = jnp.zeros((1, width), jnp.int32)
        for t in range(cap):
            line = jnp.where(lax.rem(slot, cap) == t, rows_ref[k * cap + t], line)
        seg_out[k] = line
    for j in range(1, ncol):
        peer, where = col_at(j)
        remote(seg_out.at[peer], seg_in.at[c], seg_send.at[peer], seg_recv.at[c], where).start()
    seg_in[c] = seg_out[c]

    corr = lax.dot_general(basis[...], basis[...], NT, preferred_element_type=F32)
    band = corr_col.shape[1]
    lanes = corr_col.shape[2]
    folds = -(-krylov // band)
    corr = jnp.pad(corr, ((0, folds * band - krylov), (0, 0)))
    corr_col[c] = jnp.concatenate(
        [corr[i * band : (i + 1) * band] for i in range(folds)] + [jnp.zeros((band, lanes - folds * krylov), F32)], axis=1
    )
    for j in range(1, ncol):
        peer, where = col_at(j)
        remote(corr_col.at[c], corr_col.at[c], cc_send.at[peer], cc_recv.at[c], where).start()

    def relay(m):
        series_copy(m, mate, mate).wait_recv()
        for other in others:
            pass_on(m, mate, 1, other, other).start()
        for other in others:
            series_copy(m, other, other).wait_recv()
            pass_on(m, other, 0, mate, other).start()

    def relayed(m):
        for other in others:
            far = other + 1 - 2 * side
            pass_on(m, far, 0, mate, far).wait_recv()
            pass_on(m, far, 1, other, far).wait_recv()

    for m in range(kinds):
        relay(m)
    for j in range(1, ncol):
        peer, where = col_at(j)
        remote(corr_col.at[c], corr_col.at[peer], cc_send.at[peer], cc_recv.at[peer], where).wait_recv()
    corr_row[r] = jnp.sum(corr_col[...], axis=0)
    for j in range(1, nrow):
        peer, where = row_at(j)
        remote(corr_row.at[r], corr_row.at[r], cr_send.at[peer], cr_recv.at[r], where).start()
    for m in range(kinds):
        relayed(m)

    def products(k, dst):
        for m in range(kinds):
            chunk_copy(m, k).wait()
        for t in range(cap):
            g = k * cap + t
            at = picks_ref[g]
            x = jnp.concatenate([cols[m, at] for m in range(kinds)], axis=1)
            w = jnp.concatenate([tiles[m, g] for m in range(kinds)], axis=1)
            dst[k, t] = lax.dot_general(x, w, NT, preferred_element_type=F32).astype(BF16)

    def box_copy(k, where):
        return remote(outbox.at[k], inbox.at[c], box_send.at[k], box_recv.at[c], where)

    def chunk(j, carry):
        k, where = col_at(j)
        products(k, outbox)
        box_copy(k, where).start()
        return carry

    lax.fori_loop(1, ncol, chunk, 0)
    products(c, inbox)

    for j in range(1, ncol):
        peer, where = col_at(j)
        remote(seg_out.at[peer], seg_in.at[peer], seg_send.at[peer], seg_recv.at[peer], where).wait_recv()
    line = seg_in[0]
    for k in range(1, ncol):
        line = jnp.where(lax.div(slot, cap) == k, seg_in[k], line)
    here = lax.broadcasted_iota(jnp.int32, (region, tpd), 0) + c * region
    onehot = (line[:, :tpd] == here).astype(F32).astype(BF16)

    for j in range(1, nrow):
        peer, where = row_at(j)
        remote(corr_row.at[r], corr_row.at[peer], cr_send.at[peer], cr_recv.at[peer], where).wait_recv()
    corr = jnp.sum(corr_row[...], axis=0) / entries
    corr = jnp.concatenate([corr[:, i * krylov : (i + 1) * krylov] for i in range(folds)], axis=0)[:krylov]
    eye = (
        lax.broadcasted_iota(jnp.int32, (krylov, krylov), 0) == lax.broadcasted_iota(jnp.int32, (krylov, krylov), 1)
    ).astype(F32)
    once = eye - corr
    both = eye + once
    kern = exact(both, eye + exact(once, once))

    for j in range(1, ncol):
        peer, where = col_at(j)
        remote(outbox.at[peer], inbox.at[peer], box_send.at[peer], box_recv.at[peer], where).wait_recv()
    spread[...] = inbox[...].astype(F32).reshape(tpd, bs, tile)
    for b in range(bs):
        app[:, b, :] = jnp.dot(onehot, spread[:, b, :].astype(BF16), preferred_element_type=F32)
    applied = jnp.concatenate([app[s] for s in range(region)], axis=1)

    split = pieces(applied)
    raw = fold(lax.dot_general(split, basis[...], NT, preferred_element_type=F32), bs)
    energy = fold(lax.dot_general(split, split, NT, preferred_element_type=F32), bs)
    energy = energy[:, :bs] + energy[:, bs : 2 * bs] + energy[:, 2 * bs :]
    tail_col[c] = jnp.concatenate([raw, energy, jnp.zeros((bs, 128 - krylov - bs), F32)], axis=1)
    for j in range(1, ncol):
        peer, where = col_at(j)
        remote(tail_col.at[c], tail_col.at[c], tc_send.at[peer], tc_recv.at[c], where).start()
    for j in range(1, ncol):
        peer, where = col_at(j)
        remote(tail_col.at[c], tail_col.at[peer], tc_send.at[peer], tc_recv.at[peer], where).wait_recv()
    tail_row[r] = jnp.sum(tail_col[...], axis=0)
    for j in range(1, nrow):
        peer, where = row_at(j)
        remote(tail_row.at[r], tail_row.at[r], tr_send.at[peer], tr_recv.at[r], where).start()
    for j in range(1, nrow):
        peer, where = row_at(j)
        remote(tail_row.at[r], tail_row.at[peer], tr_send.at[peer], tr_recv.at[peer], where).wait_recv()
    total = jnp.sum(tail_row[...], axis=0)

    first = total[:, :krylov] * inverse_root
    coefficients = exact(first, both)
    gram = (total[:, krylov : krylov + bs] - exact(exact(first, kern), first, NT)) / entries
    coef_ref[...] = coefficients

    sub = lax.broadcasted_iota(jnp.int32, (bs, bs), 0)
    lane = lax.broadcasted_iota(jnp.int32, (bs, bs), 1)
    up = lax.broadcasted_iota(jnp.int32, (bs, 1), 0)
    factor = jnp.zeros((bs, bs), F32)
    inverse = jnp.zeros((bs, 1), F32)
    steps = []
    for j in range(bs):
        column, line = gram[:, j : j + 1], gram[j : j + 1, :]
        pivot = jnp.sqrt(gram[j : j + 1, j : j + 1])
        column = jnp.where(up >= j, column / pivot, 0.0)
        factor = jnp.where(lane == j, column, factor)
        inverse = jnp.where(up == j, 1.0 / pivot, inverse)
        steps.append(jnp.where(up > j, column, 0.0))
        gram = gram - column * (line / pivot)
    factor_ref[...] = factor

    cleaned = applied - fold(
        jnp.dot(pieces(coefficients * inverse_root), basis[...], preferred_element_type=F32), bs
    )
    solved = cleaned * inverse
    for j in range(bs - 1):
        solved = solved - (steps[j] * inverse) * solved[j : j + 1, :]
    new_ref[...] = solved

    for m in range(kinds):
        for peer in direct:
            series_copy(m, r, peer).wait_send()
        for other in others:
            pass_on(m, mate, 1, other, other).wait_send()
            pass_on(m, other, 0, mate, other).wait_send()
    for j in range(1, ncol):
        peer, where = col_at(j)
        remote(seg_out.at[peer], seg_in.at[c], seg_send.at[peer], seg_recv.at[c], where).wait_send()
        remote(corr_col.at[c], corr_col.at[c], cc_send.at[peer], cc_recv.at[c], where).wait_send()
        box_copy(peer, where).wait_send()
        remote(tail_col.at[c], tail_col.at[c], tc_send.at[peer], tc_recv.at[c], where).wait_send()
    for j in range(1, nrow):
        peer, where = row_at(j)
        remote(corr_row.at[r], corr_row.at[r], cr_send.at[peer], cr_recv.at[r], where).wait_send()
        remote(tail_row.at[r], tail_row.at[r], tr_send.at[peer], tr_recv.at[r], where).wait_send()


def shards(basis, expand, tiles, tile_rows, tile_cols):
    nrow = lax.axis_size("row")
    ncol = lax.axis_size("col")
    krylov, length = basis.shape
    kinds, tpd, tile, _ = tiles.shape
    bs = expand.shape[1]
    region = length // tile
    cap = tpd // ncol
    width = -(-tpd // 128) * 128
    dma = pltpu.SemaphoreType.DMA
    band = 16
    lanes = -(-(-(-krylov // band) * krylov) // 128) * 128
    vmem, hbm = pl.BlockSpec(memory_space=pltpu.VMEM), pl.BlockSpec(memory_space=pltpu.HBM)
    return pl.pallas_call(
        functools.partial(kernel, nrow, ncol),
        out_shape=(
            jax.ShapeDtypeStruct((bs, length), F32),
            jax.ShapeDtypeStruct((bs, krylov), F32),
            jax.ShapeDtypeStruct((bs, bs), F32),
        ),
        in_specs=[hbm] * 5,
        out_specs=(vmem, vmem, vmem),
        scratch_shapes=[
            pltpu.VMEM(expand.shape, F32),
            pltpu.SMEM((tpd,), jnp.int32),
            pltpu.SMEM((tpd,), jnp.int32),
            pltpu.VMEM((krylov, length), BF16),
            pltpu.VMEM((kinds, tpd, tile, tile), BF16),
            pltpu.VMEM((kinds, nrow * region, bs, tile), BF16),
            pltpu.VMEM((ncol, cap, bs, tile), BF16),
            pltpu.VMEM((ncol, cap, bs, tile), BF16),
            pltpu.VMEM((ncol, 1, width), jnp.int32),
            pltpu.VMEM((ncol, 1, width), jnp.int32),
            pltpu.VMEM((ncol, band, lanes), F32),
            pltpu.VMEM((nrow, band, lanes), F32),
            pltpu.VMEM((ncol, bs, 128), F32),
            pltpu.VMEM((nrow, bs, 128), F32),
            pltpu.VMEM((tpd, bs, tile), F32),
            pltpu.VMEM((region, bs, tile), F32),
            dma((3,)),
            dma,
            dma((kinds, ncol)),
            dma((kinds, nrow)),
            dma((kinds, nrow)),
            dma((kinds, nrow, 2)),
            dma((kinds, nrow, 2)),
            dma((ncol,)),
            dma((ncol,)),
            dma((ncol,)),
            dma((ncol,)),
            dma((ncol,)),
            dma((ncol,)),
            dma((nrow,)),
            dma((nrow,)),
            dma((ncol,)),
            dma((ncol,)),
            dma((nrow,)),
            dma((nrow,)),
        ],
        compiler_params=pltpu.CompilerParams(
            collective_id=0, has_side_effects=True, vmem_limit_bytes=48 * 1024 * 1024
        ),
    )(*(pltpu.with_memory_space_constraint(x, pltpu.HBM) for x in (expand, tile_rows, tile_cols, basis, tiles)))


def solution(mesh):
    return jax.shard_map(
        shards,
        mesh=mesh,
        in_specs=(
            P(None, ("row", "col")),
            P(),
            P(None, ("row", "col"), None, None),
            P(("row", "col")),
            P(("row", "col")),
        ),
        out_specs=(P(None, ("row", "col")), P(), P()),
        check_vma=False,
    )
```

profile of v0, /device:TPU:0, one launch (start us, length us, event | category | flops | bytes accessed | tf_op | source)
XLA Modules:
  0.0 36.5 jit_solution(925287348055365405)
XLA Ops:
  0.6 34.0 %shard_map.76 = (f32[8,4096]{1,0:T(8,128)S(1)}, f32[8,40]{1,0:T(8,128)S(1)}, f32[8,8]{1,0:T(8,128)S(1)}) custom-call(f32[3,8,40]{2,1,0:T(8,128)} %expand_hbm.1, s32[96]{0:T(128)} %rows_hbm.1, s32[96]{0:T(128)} %picks_hbm.1, bf16[40,4096]{1,0:T(8,128)(2,1)} %basis_hbm.1, bf16[3,96,128,128]{3,2,1,0:T(8,128)(2,1)} %tiles_hbm.1), custom_call_target="tpu_custom_call" | custom-call | tf_op jit(solution)/shard_map/pallas_call | solution.py:338
  34.7 0.7 %copy.11 = f32[8,4096]{1,0:T(8,128)} copy(f32[8,4096]{1,0:T(8,128)S(1)} %get-tuple-element.6) | data formatting | bytes 262144
  35.3 0.6 %copy.12 = f32[8,40]{1,0:T(8,128)} copy(f32[8,40]{1,0:T(8,128)S(1)} %get-tuple-element.7) | data formatting | bytes 2560
  35.9 0.6 %copy.13 = f32[8,8]{1,0:T(8,128)} copy(f32[8,8]{1,0:T(8,128)S(1)} %get-tuple-element.8) | data formatting | bytes 512
where the time goes:
time: 36.8 us; the launch traced here: 36.5 us
  Pallas kernels  34 us (92%)
  local copies, waits for them, and re-layouts  1.84 us (5%)
  between operations  0.64 us (2%)
    pallas_call x1, Pallas kernels, shards(): pl.pallas_call(functools.partial(kernel, nrow, ncol), out_shape=(jax.Shap...  34 us
    unnamed x3, local copies, waits for them, and re-layouts  1.84 us

commit v1 on v0

--- a/solution.py
+++ b/solution.py
@@ -61,7 +61,6 @@
     tile_sem,
     ser_send,
     ser_recv,
-    fwd_send,
     fwd_recv,
     seg_send,
     seg_recv,
@@ -96,15 +95,6 @@
     for copy in small:
         copy.start()
 
-    def chunk_copy(m, k):
-        part = pl.ds(k * cap, cap)
-        return pltpu.make_async_copy(tiles_hbm.at[m, part], tiles.at[m, part], tile_sem.at[m, k])
-
-    for j in range(1, ncol + 1):
-        k = lax.rem(c + j, ncol)
-        for m in range(kinds):
-            chunk_copy(m, k).start()
-
     barrier = pltpu.get_barrier_semaphore()
     for j in range(1, nrow):
         pl.semaphore_signal(barrier, inc=1, device_id={"row": lax.rem(r + j, nrow)}, device_id_type=pl.DeviceIdType.MESH)
@@ -117,6 +107,10 @@
             device_id=where, device_id_type=pl.DeviceIdType.MESH,
         )
 
+    def landed(ref, sem):
+        part = ref.at[pl.ds(0, ref.shape[0] - 1)]
+        pltpu.make_async_copy(part, part, sem).wait()
+
     def row_at(j):
         peer = lax.rem(r + j, nrow)
         return peer, {"row": peer}
@@ -125,9 +119,13 @@
         peer = lax.rem(c + j, ncol)
         return peer, {"col": peer}
 
-    for copy in small:
-        copy.wait()
+    small[0].wait()
     load_basis.wait()
+    for m in range(kinds):
+        for k in range(ncol):
+            part = pl.ds(k * cap, cap)
+            pltpu.make_async_copy(tiles_hbm.at[m, part], tiles.at[m, part], tile_sem.at[m]).start()
+
     expand = pieces(expand_ref[...].reshape(kinds * bs, krylov))
     for l in range(region):
         part = fold(jnp.dot(expand, basis[:, l * tile : (l + 1) * tile], preferred_element_type=F32), kinds * bs)
@@ -139,21 +137,26 @@
     outer = nrow // 2
     side, pair = lax.rem(r, 2), lax.div(r, 2)
     mate = r + 1 - 2 * side
-    others = [2 * lax.rem(pair + j, outer) + side for j in range(1, outer)]
     half = region // 2
 
-    def series_copy(m, owner, peer):
+    def other(j):
+        return 2 * lax.rem(pair + j, outer) + side
+
+    def series_copy(m, owner, peer, slot):
         block = cols.at[m, pl.ds(owner * region, region)]
-        return remote(block, block, ser_send.at[m, peer], ser_recv.at[m, owner], {"row": peer})
+        return remote(block, block, ser_send, ser_recv.at[m, slot], {"row": peer})
 
     def pass_on(m, owner, h, peer, slot):
         block = cols.at[m, pl.ds(owner * region + h * half, half)]
-        return remote(block, block, fwd_send.at[m, slot, h], fwd_recv.at[m, owner, h], {"row": peer})
-
-    direct = [mate] + others
-    for m in range(kinds):
-        for peer in direct:
-            series_copy(m, r, peer).start()
+        return remote(block, block, ser_send, fwd_recv.at[m, h, slot - 1], {"row": peer})
+
+    for m in range(kinds):
+        series_copy(m, r, mate, 0).start()
+        for j in range(1, outer):
+            series_copy(m, r, other(j), outer - j).start()
+
+    small[1].wait()
+    small[2].wait()
 
     slot = lax.broadcasted_iota(jnp.int32, (1, width), 1)
     for k in range(ncol):
@@ -163,7 +166,7 @@
         seg_out[k] = line
     for j in range(1, ncol):
         peer, where = col_at(j)
-        remote(seg_out.at[peer], seg_in.at[c], seg_send.at[peer], seg_recv.at[c], where).start()
+        remote(seg_out.at[peer], seg_in.at[c], seg_send, seg_recv, where).start()
     seg_in[c] = seg_out[c]
 
     corr = lax.dot_general(basis[...], basis[...], NT, preferred_element_type=F32)
@@ -176,37 +179,33 @@
     )
     for j in range(1, ncol):
         peer, where = col_at(j)
-        remote(corr_col.at[c], corr_col.at[c], cc_send.at[peer], cc_recv.at[c], where).start()
+        remote(corr_col.at[c], corr_col.at[c], cc_send, cc_recv, where).start()
 
     def relay(m):
-        series_copy(m, mate, mate).wait_recv()
-        for other in others:
-            pass_on(m, mate, 1, other, other).start()
-        for other in others:
-            series_copy(m, other, other).wait_recv()
-            pass_on(m, other, 0, mate, other).start()
+        series_copy(m, mate, mate, 0).wait_recv()
+        for j in range(1, outer):
+            pass_on(m, mate, 1, other(j), outer - j).start()
+        for j in range(1, outer):
+            series_copy(m, other(j), other(j), j).wait_recv()
+            pass_on(m, other(j), 0, mate, j).start()
 
     def relayed(m):
-        for other in others:
-            far = other + 1 - 2 * side
-            pass_on(m, far, 0, mate, far).wait_recv()
-            pass_on(m, far, 1, other, far).wait_recv()
+        for j in range(1, outer):
+            far = other(j) + 1 - 2 * side
+            pass_on(m, far, 0, mate, j).wait_recv()
+            pass_on(m, far, 1, mate, j).wait_recv()
 
     for m in range(kinds):
         relay(m)
-    for j in range(1, ncol):
-        peer, where = col_at(j)
-        remote(corr_col.at[c], corr_col.at[peer], cc_send.at[peer], cc_recv.at[peer], where).wait_recv()
+    landed(corr_col, cc_recv)
     corr_row[r] = jnp.sum(corr_col[...], axis=0)
     for j in range(1, nrow):
         peer, where = row_at(j)
-        remote(corr_row.at[r], corr_row.at[r], cr_send.at[peer], cr_recv.at[r], where).start()
+        remote(corr_row.at[r], corr_row.at[r], cr_send, cr_recv, where).start()
     for m in range(kinds):
         relayed(m)
 
     def products(k, dst):
-        for m in range(kinds):
-            chunk_copy(m, k).wait()
         for t in range(cap):
             g = k * cap + t
             at = picks_ref[g]
@@ -215,7 +214,7 @@
             dst[k, t] = lax.dot_general(x, w, NT, preferred_element_type=F32).astype(BF16)
 
     def box_copy(k, where):
-        return remote(outbox.at[k], inbox.at[c], box_send.at[k], box_recv.at[c], where)
+        return remote(outbox.at[k], inbox.at[c], box_send, box_recv, where)
 
     def chunk(j, carry):
         k, where = col_at(j)
@@ -223,21 +222,19 @@
         box_copy(k, where).start()
         return carry
 
+    for m in range(kinds):
+        pltpu.make_async_copy(tiles_hbm.at[m], tiles.at[m], tile_sem.at[m]).wait()
     lax.fori_loop(1, ncol, chunk, 0)
     products(c, inbox)
 
-    for j in range(1, ncol):
-        peer, where = col_at(j)
-        remote(seg_out.at[peer], seg_in.at[peer], seg_send.at[peer], seg_recv.at[peer], where).wait_recv()
+    landed(seg_in, seg_recv)
     line = seg_in[0]
     for k in range(1, ncol):
         line = jnp.where(lax.div(slot, cap) == k, seg_in[k], line)
     here = lax.broadcasted_iota(jnp.int32, (region, tpd), 0) + c * region
     onehot = (line[:, :tpd] == here).astype(F32).astype(BF16)
 
-    for j in range(1, nrow):
-        peer, where = row_at(j)
-        remote(corr_row.at[r], corr_row.at[peer], cr_send.at[peer], cr_recv.at[peer], where).wait_recv()
+    landed(corr_row, cr_recv)
     corr = jnp.sum(corr_row[...], axis=0) / entries
     corr = jnp.concatenate([corr[:, i * krylov : (i + 1) * krylov] for i in range(folds)], axis=0)[:krylov]
     eye = (
@@ -247,9 +244,7 @@
     both = eye + once
     kern = exact(both, eye + exact(once, once))
 
-    for j in range(1, ncol):
-        peer, where = col_at(j)
-        remote(outbox.at[peer], inbox.at[peer], box_send.at[peer], box_recv.at[peer], where).wait_recv()
+    landed(inbox, box_recv)
     spread[...] = inbox[...].astype(F32).reshape(tpd, bs, tile)
     for b in range(bs):
         app[:, b, :] = jnp.dot(onehot, spread[:, b, :].astype(BF16), preferred_element_type=F32)
@@ -262,17 +257,13 @@
     tail_col[c] = jnp.concatenate([raw, energy, jnp.zeros((bs, 128 - krylov - bs), F32)], axis=1)
     for j in range(1, ncol):
         peer, where = col_at(j)
-        remote(tail_col.at[c], tail_col.at[c], tc_send.at[peer], tc_recv.at[c], where).start()
-    for j in range(1, ncol):
-        peer, where = col_at(j)
-        remote(tail_col.at[c], tail_col.at[peer], tc_send.at[peer], tc_recv.at[peer], where).wait_recv()
+        remote(tail_col.at[c], tail_col.at[c], tc_send, tc_recv, where).start()
+    landed(tail_col, tc_recv)
     tail_row[r] = jnp.sum(tail_col[...], axis=0)
     for j in range(1, nrow):
         peer, where = row_at(j)
-        remote(tail_row.at[r], tail_row.at[r], tr_send.at[peer], tr_recv.at[r], where).start()
-    for j in range(1, nrow):
-        peer, where = row_at(j)
-        remote(tail_row.at[r], tail_row.at[peer], tr_send.at[peer], tr_recv.at[peer], where).wait_recv()
+        remote(tail_row.at[r], tail_row.at[r], tr_send, tr_recv, where).start()
+    landed(tail_row, tr_recv)
     total = jnp.sum(tail_row[...], axis=0)
 
     first = total[:, :krylov] * inverse_root
@@ -304,22 +295,23 @@
         solved = solved - (steps[j] * inverse) * solved[j : j + 1, :]
     new_ref[...] = solved
 
-    for m in range(kinds):
-        for peer in direct:
-            series_copy(m, r, peer).wait_send()
-        for other in others:
-            pass_on(m, mate, 1, other, other).wait_send()
-            pass_on(m, other, 0, mate, other).wait_send()
-    for j in range(1, ncol):
-        peer, where = col_at(j)
-        remote(seg_out.at[peer], seg_in.at[c], seg_send.at[peer], seg_recv.at[c], where).wait_send()
-        remote(corr_col.at[c], corr_col.at[c], cc_send.at[peer], cc_recv.at[c], where).wait_send()
-        box_copy(peer, where).wait_send()
-        remote(tail_col.at[c], tail_col.at[c], tc_send.at[peer], tc_recv.at[c], where).wait_send()
-    for j in range(1, nrow):
-        peer, where = row_at(j)
-        remote(corr_row.at[r], corr_row.at[r], cr_send.at[peer], cr_recv.at[r], where).wait_send()
-        remote(tail_row.at[r], tail_row.at[r], tr_send.at[peer], tr_recv.at[r], where).wait_send()
+    sent = cols.at[:, pl.ds(0, (nrow - 1) * region)]
+    pltpu.make_async_copy(sent, sent, ser_send).wait()
+    for ref, sem in (
+        (seg_in, seg_send), (corr_col, cc_send), (inbox, box_send), (tail_col, tc_send), (corr_row, cr_send), (tail_row, tr_send)
+    ):
+        landed(ref, sem)
+
+
+def leave(new_ref, coef_ref, factor_ref, new_hbm, coef_hbm, factor_hbm, sem):
+    copies = [
+        pltpu.make_async_copy(src, dst, sem.at[i])
+        for i, (src, dst) in enumerate(((new_ref, new_hbm), (coef_ref, coef_hbm), (factor_ref, factor_hbm)))
+    ]
+    for copy in copies:
+        copy.start()
+    for copy in copies:
+        copy.wait()
 
 
 def shards(basis, expand, tiles, tile_rows, tile_cols):
@@ -335,13 +327,14 @@
     band = 16
     lanes = -(-(-(-krylov // band) * krylov) // 128) * 128
     vmem, hbm = pl.BlockSpec(memory_space=pltpu.VMEM), pl.BlockSpec(memory_space=pltpu.HBM)
-    return pl.pallas_call(
+    shapes = (
+        jax.ShapeDtypeStruct((bs, length), F32),
+        jax.ShapeDtypeStruct((bs, krylov), F32),
+        jax.ShapeDtypeStruct((bs, bs), F32),
+    )
+    held = pl.pallas_call(
         functools.partial(kernel, nrow, ncol),
-        out_shape=(
-            jax.ShapeDtypeStruct((bs, length), F32),
-            jax.ShapeDtypeStruct((bs, krylov), F32),
-            jax.ShapeDtypeStruct((bs, bs), F32),
-        ),
+        out_shape=shapes,
         in_specs=[hbm] * 5,
         out_specs=(vmem, vmem, vmem),
         scratch_shapes=[
@@ -363,28 +356,23 @@
             pltpu.VMEM((region, bs, tile), F32),
             dma((3,)),
             dma,
-            dma((kinds, ncol)),
-            dma((kinds, nrow)),
-            dma((kinds, nrow)),
-            dma((kinds, nrow, 2)),
-            dma((kinds, nrow, 2)),
-            dma((ncol,)),
-            dma((ncol,)),
-            dma((ncol,)),
-            dma((ncol,)),
-            dma((ncol,)),
-            dma((ncol,)),
-            dma((nrow,)),
-            dma((nrow,)),
-            dma((ncol,)),
-            dma((ncol,)),
-            dma((nrow,)),
-            dma((nrow,)),
-        ],
+            dma((kinds,)),
+            dma,
+            dma((kinds, nrow // 2)),
+            dma((kinds, 2, nrow // 2 - 1)),
+        ]
+        + [dma] * 12,
         compiler_params=pltpu.CompilerParams(
             collective_id=0, has_side_effects=True, vmem_limit_bytes=48 * 1024 * 1024
         ),
     )(*(pltpu.with_memory_space_constraint(x, pltpu.HBM) for x in (expand, tile_rows, tile_cols, basis, tiles)))
+    return pl.pallas_call(
+        leave,
+        out_shape=shapes,
+        in_specs=[vmem] * 3,
+        out_specs=(hbm, hbm, hbm),
+        scratch_shapes=[dma((3,))],
+    )(*(pltpu.with_memory_space_constraint(x, pltpu.VMEM) for x in held))
 
 
 def solution(mesh):

time: 36.8 us -> 33.4 us (0.908)
  local copies, waits for them, and re-layouts: 1.84 us -> 0 us
  Pallas kernels: 34 us -> 32.5 us
    unnamed x3 -> x0, local copies, waits for them, and re-layouts: 1.84 us -> none
    pallas_call x1 -> x2, Pallas kernels: 34 us -> 32.5 us  [the longest x1 31.8 us: shards(): pl.pallas_call(functools.partial(kernel, nrow, ncol), out_shape=shapes, i...]
where the time goes in v1:
time: 33.4 us; the launch traced here: 33.1 us
  Pallas kernels  32.5 us (97%)
  between operations  0.64 us (2%)
    pallas_call x1, Pallas kernels, shards(): pl.pallas_call(functools.partial(kernel, nrow, ncol), out_shape=shapes, i...  31.8 us
    pallas_call x1, Pallas kernels, shards(): pl.pallas_call(leave, out_shape=shapes, in_specs=[vmem] * 3, out_specs=(h...  0.69 us

profile of v1, /device:TPU:0, one launch (start us, length us, event | category | flops | bytes accessed | tf_op | source)
XLA Modules:
  0.0 33.1 jit_solution(18328220557098238357)
XLA Ops:
  0.6 31.8 %shard_map.76 = (f32[8,4096]{1,0:T(8,128)S(1)}, f32[8,40]{1,0:T(8,128)S(1)}, f32[8,8]{1,0:T(8,128)S(1)}) custom-call(f32[3,8,40]{2,1,0:T(8,128)} %expand_hbm.1, s32[96]{0:T(128)} %rows_hbm.1, s32[96]{0:T(128)} %picks_hbm.1, bf16[40,4096]{1,0:T(8,128)(2,1)} %basis_hbm.1, bf16[3,96,128,128]{3,2,1,0:T(8,128)(2,1)} %tiles_hbm.1), custom_call_target="tpu_custom_call" | custom-call | tf_op jit(solution)/shard_map/pallas_call | solution.py:335
  32.4 0.7 %shard_map.77 = (f32[8,4096]{1,0:T(8,128)}, f32[8,40]{1,0:T(8,128)}, f32[8,8]{1,0:T(8,128)}) custom-call(f32[8,4096]{1,0:T(8,128)S(1)} %get-tuple-element.6.new_ref, f32[8,40]{1,0:T(8,128)S(1)} %get-tuple-element.7.coef_ref, f32[8,8]{1,0:T(8,128)S(1)} %get-tuple-element.8.factor_ref), custom_call_target="tpu_custom_call" | custom-call | tf_op jit(solution)/shard_map/pallas_call | solution.py:369

commit v2 on v1

v2 whole, which is shorter than its diff:
```python
import functools
import math

import jax
import jax.numpy as jnp
from jax import lax
from jax.experimental import pallas as pl
from jax.experimental.pallas import tpu as pltpu
from jax.sharding import PartitionSpec as P

F32 = jnp.float32
BF16 = jnp.bfloat16
NT = (((1,), (1,)), ((), ()))


def exact(a, b, dims=(((1,), (0,)), ((), ()))):
    return lax.dot_general(a, b, dims, precision=lax.Precision.HIGHEST, preferred_element_type=F32)


def pieces(x):
    one = x.astype(BF16).astype(F32)
    return jnp.concatenate([one, x - one], axis=0).astype(BF16)


def fold(x, rows):
    return x[:rows] + x[rows:]


def kernel(
    nrow,
    ncol,
    expand_hbm,
    rows_hbm,
    picks_hbm,
    basis_hbm,
    tiles_hbm,
    new_ref,
    coef_ref,
    factor_ref,
    expand_ref,
    rows_ref,
    picks_ref,
    basis,
    tiles,
    cols,
    outbox,
    inbox,
    seg_out,
    seg_in,
    corr_col,
    corr_row,
    tail,
    place,
    small_sem,
    basis_sem,
    tile_sem,
    ser_send,
    ser_recv,
    fwd_recv,
    seg_send,
    seg_recv,
    box_send,
    box_recv,
    cc_send,
    cc_recv,
    cr_send,
    cr_recv,
    tail_send,
    tail_recv,
    low_sem,
    high_sem,
):
    r = lax.axis_index("row")
    c = lax.axis_index("col")
    krylov, length = basis.shape
    kinds, tpd, tile, _ = tiles.shape
    cap = tpd // ncol
    region = length // tile
    bs = expand_ref.shape[1]
    entries = length * nrow * ncol
    inverse_root = 1.0 / math.sqrt(entries)
    width = seg_in.shape[2]

    load_basis = pltpu.make_async_copy(basis_hbm, basis, basis_sem)
    load_basis.start()
    small = [
        pltpu.make_async_copy(src, dst, small_sem.at[i])
        for i, (src, dst) in enumerate(((expand_hbm, expand_ref), (rows_hbm, rows_ref), (picks_hbm, picks_ref)))
    ]
    for copy in small:
        copy.start()

    outer = nrow // 2
    side, pair = lax.rem(r, 2), lax.div(r, 2)
    mate = r + 1 - 2 * side
    half = region // 2

    def other(j):
        return 2 * lax.rem(pair + j, outer) + side

    def signal(sem, where):
        pl.semaphore_signal(sem, inc=1, device_id=where, device_id_type=pl.DeviceIdType.MESH)

    barrier = pltpu.get_barrier_semaphore()
    has_low, has_high = c >= 2, c < ncol - 2
    even = c - lax.rem(c, 2)

    def low(i):
        return {"col": lax.rem(even - 2 + i + ncol, ncol)}

    def high(i):
        return {"col": lax.rem(even + 2 + i, ncol)}

    signal(barrier, {"row": mate})
    for j in range(1, outer):
        signal(barrier, {"row": other(j)})
    signal(barrier, {"col": c + 1 - 2 * lax.rem(c, 2)})
    for i in range(2):
        pl.when(has_low)(lambda: signal(barrier, low(i)))
        pl.when(has_high)(lambda: signal(barrier, high(i)))

    def tell(i):
        pl.when(has_low)(lambda: signal(high_sem.at[i], low(lax.rem(c, 2))))
        pl.when(has_high)(lambda: signal(low_sem.at[i], high(lax.rem(c, 2))))

    def hear(i):
        pl.when(has_low)(lambda: pl.semaphore_wait(low_sem.at[i], 1))
        pl.when(has_high)(lambda: pl.semaphore_wait(high_sem.at[i], 1))

    def remote(src, dst, send_sem, recv_sem, where):
        return pltpu.make_async_remote_copy(
            src_ref=src, dst_ref=dst, send_sem=send_sem, recv_sem=recv_sem,
            device_id=where, device_id_type=pl.DeviceIdType.MESH,
        )

    def landed(ref, sem):
        part = ref.at[pl.ds(0, ref.shape[0] - 1)]
        pltpu.make_async_copy(part, part, sem).wait()

    def row_at(j):
        peer = lax.rem(r + j, nrow)
        return peer, {"row": peer}

    def col_at(j):
        peer = lax.rem(c + j, ncol)
        return peer, {"col": peer}

    small[0].wait()
    load_basis.wait()
    for m in range(kinds):
        for k in range(ncol):
            part = pl.ds(k * cap, cap)
            pltpu.make_async_copy(tiles_hbm.at[m, part], tiles.at[m, part], tile_sem.at[m]).start()

    expand = pieces(expand_ref[...].reshape(kinds * bs, krylov))
    for l in range(region):
        part = fold(jnp.dot(expand, basis[:, l * tile : (l + 1) * tile], preferred_element_type=F32), kinds * bs)
        for m in range(kinds):
            cols[m, r * region + l] = part[m * bs : (m + 1) * bs].astype(BF16)

    pl.semaphore_wait(barrier, outer + 1 + 2 * (has_low.astype(jnp.int32) + has_high.astype(jnp.int32)))

    def series_copy(m, owner, peer, slot):
        block = cols.at[m, pl.ds(owner * region, region)]
        return remote(block, block, ser_send, ser_recv.at[m, slot], {"row": peer})

    def pass_on(m, owner, h, peer, slot):
        block = cols.at[m, pl.ds(owner * region + h * half, half)]
        return remote(block, block, ser_send, fwd_recv.at[m, h, slot - 1], {"row": peer})

    for m in range(kinds):
        series_copy(m, r, mate, 0).start()
        for j in range(1, outer):
            series_copy(m, r, other(j), outer - j).start()

    rounds = ncol // 2 - 2
    if rounds > 0:
        tell(0)

    small[1].wait()
    small[2].wait()
    slot = lax.broadcasted_iota(jnp.int32, (1, width), 1)
    entry, inner = lax.rem(lax.div(slot, bs), cap), lax.rem(slot, bs)
    for k in range(ncol):
        line = jnp.zeros((1, width), jnp.int32)
        for t in range(cap):
            line = jnp.where(entry == t, rows_ref[k * cap + t] * bs, line)
        seg_out[k] = line + inner
    seg_in[c] = seg_out[c]

    corr = lax.dot_general(basis[...], basis[...], NT, preferred_element_type=F32)
    band = corr_col.shape[1]
    lanes = corr_col.shape[2]
    folds = -(-krylov // band)
    corr = jnp.pad(corr, ((0, folds * band - krylov), (0, 0)))
    corr_col[c] = jnp.concatenate(
        [corr[i * band : (i + 1) * band] for i in range(folds)] + [jnp.zeros((band, lanes - folds * krylov), F32)], axis=1
    )

    def relay(m):
        series_copy(m, mate, mate, 0).wait_recv()
        for j in range(1, outer):
            pass_on(m, mate, 1, other(j), outer - j).start()
        for j in range(1, outer):
            series_copy(m, other(j), other(j), j).wait_recv()
            pass_on(m, other(j), 0, mate, j).start()

    def relayed(m):
        for j in range(1, outer):
            far = other(j) + 1 - 2 * side
            pass_on(m, far, 0, mate, j).wait_recv()
            pass_on(m, far, 1, mate, j).wait_recv()

    relay(0)
    for i in range(rounds - 1):
        hear(i)
        tell(i + 1)
    relay(1)
    if rounds > 0:
        hear(rounds - 1)
    for j in range(1, ncol):
        peer, where = col_at(j)
        remote(seg_out.at[peer], seg_in.at[c], seg_send, seg_recv, where).start()
    for j in range(1, ncol):
        peer, where = col_at(j)
        remote(corr_col.at[c], corr_col.at[c], cc_send, cc_recv, where).start()
    for m in range(2, kinds):
        relay(m)
    for m in range(kinds):
        relayed(m)

    def products(k, dst):
        for t in range(0, cap, 2):
            both = []
            for g in (k * cap + t, k * cap + t + 1):
                at = picks_ref[g]
                x = jnp.concatenate([cols[m, at] for m in range(kinds)], axis=1)
                w = jnp.concatenate([tiles[m, g] for m in range(kinds)], axis=1)
                both.append(lax.dot_general(x, w, NT, preferred_element_type=F32))
            dst[k, t * bs : (t + 2) * bs] = jnp.concatenate(both, axis=0).astype(BF16)

    def box_copy(k, where):
        return remote(outbox.at[k], inbox.at[c], box_send, box_recv, where)

    def chunk(j, carry):
        k, where = col_at(j)
        products(k, outbox)
        box_copy(k, where).start()
        return carry

    for m in range(kinds):
        pltpu.make_async_copy(tiles_hbm.at[m], tiles.at[m], tile_sem.at[m]).wait()
    lax.fori_loop(1, ncol, chunk, 0)
    products(c, inbox)

    landed(corr_col, cc_recv)
    corr_row[r] = jnp.sum(corr_col[...], axis=0)
    for j in range(1, nrow):
        peer, where = row_at(j)
        remote(corr_row.at[r], corr_row.at[r], cr_send, cr_recv, where).start()
    landed(seg_in, seg_recv)
    line = seg_in[0]
    for k in range(1, ncol):
        line = jnp.where(lax.div(slot, cap * bs) == k, seg_in[k], line)
    here = lax.broadcasted_iota(jnp.int32, (region * bs, tpd * bs), 0) + c * (region * bs)
    place[...] = (line[:, : tpd * bs] == here).astype(F32).astype(BF16)

    landed(inbox, box_recv)
    app = jnp.dot(place[...], inbox[...].reshape(tpd * bs, tile), preferred_element_type=F32)
    applied = jnp.concatenate([app[s * bs : (s + 1) * bs] for s in range(region)], axis=1)

    split = pieces(applied)
    stack = jnp.concatenate([split, basis[...]], axis=0)
    raw = fold(lax.dot_general(split, stack, NT, preferred_element_type=F32), bs)
    raw = jnp.concatenate([raw, jnp.zeros((bs, 64 - 2 * bs - krylov), F32)], axis=1)
    me = r * ncol + c
    tail[me] = jnp.concatenate([raw[: bs // 2], raw[bs // 2 :]], axis=1)

    for j in sorted(range(ncol), key=lambda j: -min(j, ncol - j)):
        for i in reversed(range(nrow)):
            if i or j:
                where = {"row": lax.rem(r + i, nrow), "col": lax.rem(c + j, ncol)}
                remote(tail.at[me], tail.at[me], tail_send, tail_recv, where).start()

    landed(corr_row, cr_recv)
    corr = jnp.sum(corr_row[...], axis=0) / entries
    corr = jnp.concatenate([corr[:, i * krylov : (i + 1) * krylov] for i in range(folds)], axis=0)[:krylov]
    eye = (
        lax.broadcasted_iota(jnp.int32, (krylov, krylov), 0) == lax.broadcasted_iota(jnp.int32, (krylov, krylov), 1)
    ).astype(F32)
    once = eye - corr
    both = eye + once
    kern = exact(both, eye + exact(once, once)) * (inverse_root / entries * inverse_root)
    before, after = 2 * bs, 64 - 2 * bs - krylov
    both = jnp.pad(both * inverse_root, ((before, after), (0, 0)))
    kern = jnp.pad(kern, ((before, after), (before, after)))
    down, along = (lax.broadcasted_iota(jnp.int32, (64, bs), d) for d in (0, 1))
    gather = ((down == along) | (down == along + bs)).astype(F32)

    landed(tail, tail_recv)

    total = jnp.sum(tail[...], axis=0)
    total = jnp.concatenate([total[:, :64], total[:, 64:]], axis=0)
    gram = exact(total, gather) / entries - exact(exact(total, kern), total, NT)
    coefficients = exact(total, both)
    coef_ref[...] = coefficients

    sub = lax.broadcasted_iota(jnp.int32, (bs, tile), 0)
    lane = lax.broadcasted_iota(jnp.int32, (bs, tile), 1)
    columns = [jnp.broadcast_to(gram[:, j : j + 1], (bs, tile)) for j in range(bs)]
    factor = jnp.zeros((bs, tile), F32)
    inverse = jnp.zeros((bs, tile), F32)
    for j in range(bs):
        root = jnp.broadcast_to(lax.rsqrt(columns[j][j : j + 1]), (bs, tile))
        column = jnp.where(sub >= j, columns[j] * root, 0.0)
        for k in range(j + 1, bs):
            columns[k] = columns[k] - column * column[k : k + 1]
        factor = jnp.where(lane == j, column, factor)
        inverse = jnp.where(sub == j, root, inverse)
        columns[j] = jnp.where(sub > j, column, 0.0)
    factor_ref[...] = factor[:, :bs]

    correction = fold(jnp.dot(pieces(coefficients * inverse_root), basis[...], preferred_element_type=F32), bs)
    steps = [columns[j] * inverse for j in range(bs - 1)]
    for s in range(region):
        part = slice(s * tile, (s + 1) * tile)
        solved = (applied[:, part] - correction[:, part]) * inverse
        for j in range(bs - 1):
            solved = solved - steps[j] * solved[j : j + 1]
        new_ref[:, part] = solved

    sent = cols.at[:, pl.ds(0, (nrow - 1) * region)]
    pltpu.make_async_copy(sent, sent, ser_send).wait()
    for ref, sem in (
        (seg_in, seg_send), (corr_col, cc_send), (inbox, box_send), (corr_row, cr_send), (tail, tail_send)
    ):
        landed(ref, sem)


def leave(new_ref, coef_ref, factor_ref, new_hbm, coef_hbm, factor_hbm, sem):
    copies = [
        pltpu.make_async_copy(src, dst, sem.at[i])
        for i, (src, dst) in enumerate(((new_ref, new_hbm), (coef_ref, coef_hbm), (factor_ref, factor_hbm)))
    ]
    for copy in copies:
        copy.start()
    for copy in copies:
        copy.wait()


def shards(basis, expand, tiles, tile_rows, tile_cols):
    nrow = lax.axis_size("row")
    ncol = lax.axis_size("col")
    krylov, length = basis.shape
    kinds, tpd, tile, _ = tiles.shape
    bs = expand.shape[1]
    region = length // tile
    cap = tpd // ncol
    width = -(-tpd * bs // 128) * 128
    dma = pltpu.SemaphoreType.DMA
    band = 16
    lanes = -(-(-(-krylov // band) * krylov) // 128) * 128
    vmem, hbm = pl.BlockSpec(memory_space=pltpu.VMEM), pl.BlockSpec(memory_space=pltpu.HBM)
    shapes = (
        jax.ShapeDtypeStruct((bs, length), F32),
        jax.ShapeDtypeStruct((bs, krylov), F32),
        jax.ShapeDtypeStruct((bs, bs), F32),
    )
    held = pl.pallas_call(
        functools.partial(kernel, nrow, ncol),
        out_shape=shapes,
        in_specs=[hbm] * 5,
        out_specs=(vmem, vmem, vmem),
        scratch_shapes=[
            pltpu.VMEM(expand.shape, F32),
            pltpu.SMEM((tpd,), jnp.int32),
            pltpu.SMEM((tpd,), jnp.int32),
            pltpu.VMEM((krylov, length), BF16),
            pltpu.VMEM((kinds, tpd, tile, tile), BF16),
            pltpu.VMEM((kinds, nrow * region, bs, tile), BF16),
            pltpu.VMEM((ncol, cap * bs, tile), BF16),
            pltpu.VMEM((ncol, cap * bs, tile), BF16),
            pltpu.VMEM((ncol, 1, width), jnp.int32),
            pltpu.VMEM((ncol, 1, width), jnp.int32),
            pltpu.VMEM((ncol, band, lanes), F32),
            pltpu.VMEM((nrow, band, lanes), F32),
            pltpu.VMEM((nrow * ncol, bs // 2, 128), F32),
            pltpu.VMEM((region * bs, tpd * bs), BF16),
            dma((3,)),
            dma,
            dma((kinds,)),
            dma,
            dma((kinds, nrow // 2)),
            dma((kinds, 2, nrow // 2 - 1)),
        ]
        + [dma] * 10
        + [pltpu.SemaphoreType.REGULAR((max(ncol // 2 - 2, 1),))] * 2,
        compiler_params=pltpu.CompilerParams(
            collective_id=0, has_side_effects=True, vmem_limit_bytes=48 * 1024 * 1024
        ),
    )(*(pltpu.with_memory_space_constraint(x, pltpu.HBM) for x in (expand, tile_rows, tile_cols, basis, tiles)))
    return pl.pallas_call(
        leave,
        out_shape=shapes,
        in_specs=[vmem] * 3,
        out_specs=(hbm, hbm, hbm),
        scratch_shapes=[dma((3,))],
    )(*(pltpu.with_memory_space_constraint(x, pltpu.VMEM) for x in held))


def solution(mesh):
    return jax.shard_map(
        shards,
        mesh=mesh,
        in_specs=(
            P(None, ("row", "col")),
            P(),
            P(None, ("row", "col"), None, None),
            P(("row", "col")),
            P(("row", "col")),
        ),
        out_specs=(P(None, ("row", "col")), P(), P()),
        check_vma=False,
    )
```

time: 33.4 us -> 28.9 us (0.87)
  Pallas kernels: 32.5 us -> 28 us
    pallas_call x1, Pallas kernels: 31.8 us -> 27.4 us  [shards(): pl.pallas_call(functools.partial(kernel, nrow, ncol), out_shape=shapes, i...]
where the time goes in v2:
time: 28.9 us; the launch traced here: 28.7 us
  Pallas kernels  28 us (97%)
  between operations  0.64 us (2%)
    pallas_call x1, Pallas kernels, shards(): pl.pallas_call(functools.partial(kernel, nrow, ncol), out_shape=shapes, i...  27.4 us
    pallas_call x1, Pallas kernels, shards(): pl.pallas_call(leave, out_shape=shapes, in_specs=[vmem] * 3, out_specs=(h...  0.69 us

profile of v2, /device:TPU:0, one launch (start us, length us, event | category | flops | bytes accessed | tf_op | source)
XLA Modules:
  0.0 28.7 jit_solution(5347259137880118428)
XLA Ops:
  0.6 27.4 %shard_map.76 = (f32[8,4096]{1,0:T(8,128)S(1)}, f32[8,40]{1,0:T(8,128)S(1)}, f32[8,8]{1,0:T(8,128)S(1)}) custom-call(f32[3,8,40]{2,1,0:T(8,128)} %expand_hbm.1, s32[96]{0:T(128)} %rows_hbm.1, s32[96]{0:T(128)} %picks_hbm.1, bf16[40,4096]{1,0:T(8,128)(2,1)} %basis_hbm.1, bf16[3,96,128,128]{3,2,1,0:T(8,128)(2,1)} %tiles_hbm.1), custom_call_target="tpu_custom_call" | custom-call | tf_op jit(solution)/shard_map/pallas_call | solution.py:369
  28.0 0.7 %shard_map.77 = (f32[8,4096]{1,0:T(8,128)}, f32[8,40]{1,0:T(8,128)}, f32[8,8]{1,0:T(8,128)}) custom-call(f32[8,4096]{1,0:T(8,128)S(1)} %get-tuple-element.6.new_ref, f32[8,40]{1,0:T(8,128)S(1)} %get-tuple-element.7.coef_ref, f32[8,8]{1,0:T(8,128)S(1)} %get-tuple-element.8.factor_ref), custom_call_target="tpu_custom_call" | custom-call | tf_op jit(solution)/shard_map/pallas_call | solution.py:402

commit v3 on v2

--- a/solution.py
+++ b/solution.py
@@ -42,7 +42,9 @@
     picks_ref,
     basis,
     tiles,
-    cols,
+    cols0,
+    cols1,
+    cols2,
     outbox,
     inbox,
     seg_out,
@@ -51,6 +53,7 @@
     corr_row,
     tail,
     place,
+    held,
     small_sem,
     basis_sem,
     tile_sem,
@@ -72,6 +75,7 @@
 ):
     r = lax.axis_index("row")
     c = lax.axis_index("col")
+    cols = (cols0, cols1, cols2)
     krylov, length = basis.shape
     kinds, tpd, tile, _ = tiles.shape
     cap = tpd // ncol
@@ -152,30 +156,36 @@
             part = pl.ds(k * cap, cap)
             pltpu.make_async_copy(tiles_hbm.at[m, part], tiles.at[m, part], tile_sem.at[m]).start()
 
-    expand = pieces(expand_ref[...].reshape(kinds * bs, krylov))
-    for l in range(region):
-        part = fold(jnp.dot(expand, basis[:, l * tile : (l + 1) * tile], preferred_element_type=F32), kinds * bs)
-        for m in range(kinds):
-            cols[m, r * region + l] = part[m * bs : (m + 1) * bs].astype(BF16)
-
-    pl.semaphore_wait(barrier, outer + 1 + 2 * (has_low.astype(jnp.int32) + has_high.astype(jnp.int32)))
+    def make(m):
+        one = pieces(expand_ref[m])
+        for l in range(region):
+            part = jnp.dot(one, basis[:, l * tile : (l + 1) * tile], preferred_element_type=F32)
+            cols[m][r * region + l] = fold(part, bs).astype(BF16)
 
     def series_copy(m, owner, peer, slot):
-        block = cols.at[m, pl.ds(owner * region, region)]
-        return remote(block, block, ser_send, ser_recv.at[m, slot], {"row": peer})
+        block = cols[m].at[pl.ds(owner * region, region)]
+        return remote(block, block, ser_send.at[m], ser_recv.at[m, slot], {"row": peer})
 
     def pass_on(m, owner, h, peer, slot):
-        block = cols.at[m, pl.ds(owner * region + h * half, half)]
-        return remote(block, block, ser_send, fwd_recv.at[m, h, slot - 1], {"row": peer})
-
-    for m in range(kinds):
+        block = cols[m].at[pl.ds(owner * region + h * half, half)]
+        return remote(block, block, ser_send.at[m], fwd_recv.at[m, h, slot - 1], {"row": peer})
+
+    def spread(m):
         series_copy(m, r, mate, 0).start()
         for j in range(1, outer):
             series_copy(m, r, other(j), outer - j).start()
 
+    make(0)
+
+    pl.semaphore_wait(barrier, outer + 1 + 2 * (has_low.astype(jnp.int32) + has_high.astype(jnp.int32)))
+    spread(0)
     rounds = ncol // 2 - 2
     if rounds > 0:
         tell(0)
+
+    for m in range(1, kinds):
+        make(m)
+        spread(m)
 
     small[1].wait()
     small[2].wait()
@@ -226,32 +236,65 @@
         remote(corr_col.at[c], corr_col.at[c], cc_send, cc_recv, where).start()
     for m in range(2, kinds):
         relay(m)
-    for m in range(kinds):
+    for m in range(kinds - 1):
         relayed(m)
-
-    def products(k, dst):
-        for t in range(0, cap, 2):
-            both = []
-            for g in (k * cap + t, k * cap + t + 1):
-                at = picks_ref[g]
-                x = jnp.concatenate([cols[m, at] for m in range(kinds)], axis=1)
-                w = jnp.concatenate([tiles[m, g] for m in range(kinds)], axis=1)
-                both.append(lax.dot_general(x, w, NT, preferred_element_type=F32))
-            dst[k, t * bs : (t + 2) * bs] = jnp.concatenate(both, axis=0).astype(BF16)
-
-    def box_copy(k, where):
-        return remote(outbox.at[k], inbox.at[c], box_send, box_recv, where)
-
-    def chunk(j, carry):
-        k, where = col_at(j)
-        products(k, outbox)
-        box_copy(k, where).start()
-        return carry
 
     for m in range(kinds):
         pltpu.make_async_copy(tiles_hbm.at[m], tiles.at[m], tile_sem.at[m]).wait()
-    lax.fori_loop(1, ncol, chunk, 0)
-    products(c, inbox)
+
+    def products(k, t, ms):
+        out = []
+        for g in (k * cap + t, k * cap + t + 1):
+            at = picks_ref[g]
+            x = jnp.concatenate([cols[m][at] for m in ms], axis=1)
+            w = jnp.concatenate([tiles[m, g] for m in ms], axis=1)
+            out.append(lax.dot_general(x, w, NT, preferred_element_type=F32))
+        return jnp.concatenate(out, axis=0)
+
+    def box_copy(k):
+        return remote(outbox.at[k], inbox.at[c], box_send, box_recv, {"col": k})
+
+    across = ncol // 2
+    mine = lax.div(c, across)
+
+    def far_side(i):
+        return (1 - mine) * across + lax.rem(c + i, across)
+
+    def near_side(i):
+        return mine * across + lax.rem(c + i, across)
+
+    early = held.shape[0]
+    for i in range(early):
+        for t in range(0, cap, 2):
+            held[i, t * bs : (t + 2) * bs] = products(far_side(i), t, range(kinds - 1))
+
+    relayed(kinds - 1)
+
+    for i in range(early):
+        k = far_side(i)
+        for t in range(0, cap, 2):
+            rows = slice(t * bs, (t + 2) * bs)
+            outbox[k, rows] = (held[i, rows] + products(k, t, (kinds - 1,))).astype(BF16)
+        box_copy(k).start()
+
+    def whole(k, dst):
+        for t in range(0, cap, 2):
+            dst[k, t * bs : (t + 2) * bs] = products(k, t, range(kinds)).astype(BF16)
+
+    def send_far(i, carry):
+        whole(far_side(i), outbox)
+        box_copy(far_side(i)).start()
+        return carry
+
+    def send_near(i, carry):
+        whole(near_side(i), outbox)
+        box_copy(near_side(i)).start()
+        return carry
+
+    lax.fori_loop(early, across, send_far, 0)
+    lax.fori_loop(1, across, send_near, 0)
+
+    whole(c, inbox)
 
     landed(corr_col, cc_recv)
     corr_row[r] = jnp.sum(corr_col[...], axis=0)
@@ -292,17 +335,35 @@
     both = eye + once
     kern = exact(both, eye + exact(once, once)) * (inverse_root / entries * inverse_root)
     before, after = 2 * bs, 64 - 2 * bs - krylov
-    both = jnp.pad(both * inverse_root, ((before, after), (0, 0)))
-    kern = jnp.pad(kern, ((before, after), (before, after)))
     down, along = (lax.broadcasted_iota(jnp.int32, (64, bs), d) for d in (0, 1))
-    gather = ((down == along) | (down == along + bs)).astype(F32)
+    gather = ((down == along) | (down == along + bs)).astype(F32) / entries
+    mix = jnp.concatenate(
+        [
+            jnp.pad(both * inverse_root, ((before, after), (0, 0))),
+            gather,
+            jnp.zeros((64, 64 + before - krylov - bs), F32),
+            jnp.pad(kern, ((before, after), (0, after))),
+        ],
+        axis=1,
+    )
+    mix = jnp.concatenate([mix, jnp.zeros((64, 128), F32)], axis=0)
+    coarse = mix.astype(BF16).astype(F32)
+    mix = jnp.concatenate([coarse, mix - coarse], axis=1).astype(BF16)
+    right = lax.broadcasted_iota(jnp.int32, (bs, 128), 1) >= 64
+    below = lax.broadcasted_iota(jnp.int32, (bs, 128), 0) >= bs // 2
 
     landed(tail, tail_recv)
 
     total = jnp.sum(tail[...], axis=0)
-    total = jnp.concatenate([total[:, :64], total[:, 64:]], axis=0)
-    gram = exact(total, gather) / entries - exact(exact(total, kern), total, NT)
-    coefficients = exact(total, both)
+    turned = jnp.concatenate([total[:, 64:], total[:, :64]], axis=1)
+    total = jnp.where(right == below, jnp.concatenate([total, total], axis=0), jnp.concatenate([turned, turned], axis=0))
+    total = pieces(total)
+    made = fold(jnp.dot(total, mix, preferred_element_type=F32), bs)
+    made = made[:, :128] + made[:, 128:]
+    taken = pieces(jnp.where(right, made, 0.0))
+    taken = fold(lax.dot_general(taken, total, NT, preferred_element_type=F32), bs)
+    gram = made[:, krylov : krylov + bs] - (taken[:, :bs] + taken[:, bs:])
+    coefficients = made[:, :krylov]
     coef_ref[...] = coefficients
 
     sub = lax.broadcasted_iota(jnp.int32, (bs, tile), 0)
@@ -329,8 +390,9 @@
             solved = solved - steps[j] * solved[j : j + 1]
         new_ref[:, part] = solved
 
-    sent = cols.at[:, pl.ds(0, (nrow - 1) * region)]
-    pltpu.make_async_copy(sent, sent, ser_send).wait()
+    for m in range(kinds):
+        sent = cols[m].at[pl.ds(0, (nrow - 1) * region)]
+        pltpu.make_async_copy(sent, sent, ser_send.at[m]).wait()
     for ref, sem in (
         (seg_in, seg_send), (corr_col, cc_send), (inbox, box_send), (corr_row, cr_send), (tail, tail_send)
     ):
@@ -377,7 +439,7 @@
             pltpu.SMEM((tpd,), jnp.int32),
             pltpu.VMEM((krylov, length), BF16),
             pltpu.VMEM((kinds, tpd, tile, tile), BF16),
-            pltpu.VMEM((kinds, nrow * region, bs, tile), BF16),
+            *[pltpu.VMEM((nrow * region, bs, tile), BF16)] * kinds,
             pltpu.VMEM((ncol, cap * bs, tile), BF16),
             pltpu.VMEM((ncol, cap * bs, tile), BF16),
             pltpu.VMEM((ncol, 1, width), jnp.int32),
@@ -386,10 +448,11 @@
             pltpu.VMEM((nrow, band, lanes), F32),
             pltpu.VMEM((nrow * ncol, bs // 2, 128), F32),
             pltpu.VMEM((region * bs, tpd * bs), BF16),
+            pltpu.VMEM((2, cap * bs, tile), F32),
             dma((3,)),
             dma,
             dma((kinds,)),
-            dma,
+            dma((kinds,)),
             dma((kinds, nrow // 2)),
             dma((kinds, 2, nrow // 2 - 1)),
         ]

time: 28.9 us -> 28.8 us (level)
  no operation moved by 1% of the time
where the time goes in v3:
time: 28.8 us; the launch traced here: 28.6 us
  Pallas kernels  27.9 us (97%)
  between operations  0.64 us (2%)
    pallas_call x1, Pallas kernels, shards(): pl.pallas_call(functools.partial(kernel, nrow, ncol), out_shape=shapes, i...  27.2 us
    pallas_call x1, Pallas kernels, shards(): pl.pallas_call(leave, out_shape=shapes, in_specs=[vmem] * 3, out_specs=(h...  0.69 us

profile of v3, /device:TPU:0, one launch (start us, length us, event | category | flops | bytes accessed | tf_op | source)
XLA Modules:
  0.0 28.6 jit_solution(4534572286017012197)
XLA Ops:
  0.6 27.2 %shard_map.76 = (f32[8,4096]{1,0:T(8,128)S(1)}, f32[8,40]{1,0:T(8,128)S(1)}, f32[8,8]{1,0:T(8,128)S(1)}) custom-call(f32[3,8,40]{2,1,0:T(8,128)} %expand_hbm.1, s32[96]{0:T(128)} %rows_hbm.1, s32[96]{0:T(128)} %picks_hbm.1, bf16[40,4096]{1,0:T(8,128)(2,1)} %basis_hbm.1, bf16[3,96,128,128]{3,2,1,0:T(8,128)(2,1)} %tiles_hbm.1), custom_call_target="tpu_custom_call" | custom-call | tf_op jit(solution)/shard_map/pallas_call | solution.py:431
  27.9 0.7 %shard_map.77 = (f32[8,4096]{1,0:T(8,128)}, f32[8,40]{1,0:T(8,128)}, f32[8,8]{1,0:T(8,128)}) custom-call(f32[8,4096]{1,0:T(8,128)S(1)} %get-tuple-element.6.new_ref, f32[8,40]{1,0:T(8,128)S(1)} %get-tuple-element.7.coef_ref, f32[8,8]{1,0:T(8,128)S(1)} %get-tuple-element.8.factor_ref), custom_call_target="tpu_custom_call" | custom-call | tf_op jit(solution)/shard_map/pallas_call | solution.py:465

commit v4 on v3

--- a/solution.py
+++ b/solution.py
@@ -162,30 +162,40 @@
             part = jnp.dot(one, basis[:, l * tile : (l + 1) * tile], preferred_element_type=F32)
             cols[m][r * region + l] = fold(part, bs).astype(BF16)
 
-    def series_copy(m, owner, peer, slot):
-        block = cols[m].at[pl.ds(owner * region, region)]
-        return remote(block, block, ser_send.at[m], ser_recv.at[m, slot], {"row": peer})
+    def block(m, owner, h):
+        return cols[m].at[pl.ds(owner * region + h * half, half)]
+
+    def series_copy(m, owner, h, peer, slot):
+        part = block(m, owner, h)
+        return remote(part, part, ser_send.at[m], ser_recv.at[m, h, slot], {"row": peer})
 
     def pass_on(m, owner, h, peer, slot):
-        block = cols[m].at[pl.ds(owner * region + h * half, half)]
-        return remote(block, block, ser_send.at[m], fwd_recv.at[m, h, slot - 1], {"row": peer})
-
-    def spread(m):
-        series_copy(m, r, mate, 0).start()
+        part = block(m, owner, h)
+        return remote(part, part, ser_send.at[m], fwd_recv.at[m, h, slot - 1], {"row": peer})
+
+    def spread(m, h):
+        series_copy(m, r, 1 - h, mate, 0).start()
         for j in range(1, outer):
-            series_copy(m, r, other(j), outer - j).start()
+            series_copy(m, r, h, other(j), outer - j).start()
 
     make(0)
 
     pl.semaphore_wait(barrier, outer + 1 + 2 * (has_low.astype(jnp.int32) + has_high.astype(jnp.int32)))
-    spread(0)
+    spread(0, 0)
     rounds = ncol // 2 - 2
     if rounds > 0:
         tell(0)
 
     for m in range(1, kinds):
         make(m)
-        spread(m)
+        spread(m, 0)
+
+    def second_halves():
+        for m in range(kinds):
+            spread(m, 1)
+
+    late = lax.rem(c, 2) == 1
+    pl.when(jnp.logical_not(late))(second_halves)
 
     small[1].wait()
     small[2].wait()
@@ -208,20 +218,24 @@
     )
 
     def relay(m):
-        series_copy(m, mate, mate, 0).wait_recv()
+        series_copy(m, mate, 1, mate, 0).wait_recv()
         for j in range(1, outer):
             pass_on(m, mate, 1, other(j), outer - j).start()
         for j in range(1, outer):
-            series_copy(m, other(j), other(j), j).wait_recv()
+            series_copy(m, other(j), 0, other(j), j).wait_recv()
             pass_on(m, other(j), 0, mate, j).start()
 
     def relayed(m):
+        series_copy(m, mate, 0, mate, 0).wait_recv()
+        for j in range(1, outer):
+            series_copy(m, other(j), 1, other(j), j).wait_recv()
         for j in range(1, outer):
             far = other(j) + 1 - 2 * side
             pass_on(m, far, 0, mate, j).wait_recv()
             pass_on(m, far, 1, mate, j).wait_recv()
 
     relay(0)
+    pl.when(late)(second_halves)
     for i in range(rounds - 1):
         hear(i)
         tell(i + 1)
@@ -453,7 +467,7 @@
             dma,
             dma((kinds,)),
             dma((kinds,)),
-            dma((kinds, nrow // 2)),
+            dma((kinds, 2, nrow // 2)),
             dma((kinds, 2, nrow // 2 - 1)),
         ]
         + [dma] * 10

time: 28.8 us -> 27.2 us (0.944)
  Pallas kernels: 27.9 us -> 26.3 us
    pallas_call x1, Pallas kernels: 27.2 us -> 25.6 us  [shards(): pl.pallas_call(functools.partial(kernel, nrow, ncol), out_shape=shapes, i...]
where the time goes in v4:
time: 27.2 us; the launch traced here: 27 us
  Pallas kernels  26.3 us (97%)
  between operations  0.64 us (2%)
    pallas_call x1, Pallas kernels, shards(): pl.pallas_call(functools.partial(kernel, nrow, ncol), out_shape=shapes, i...  25.6 us
    pallas_call x1, Pallas kernels, shards(): pl.pallas_call(leave, out_shape=shapes, in_specs=[vmem] * 3, out_specs=(h...  0.69 us

profile of v4, /device:TPU:0, one launch (start us, length us, event | category | flops | bytes accessed | tf_op | source)
XLA Modules:
  0.0 27.0 jit_solution(137688140539590663)
XLA Ops:
  0.6 25.6 %shard_map.76 = (f32[8,4096]{1,0:T(8,128)S(1)}, f32[8,40]{1,0:T(8,128)S(1)}, f32[8,8]{1,0:T(8,128)S(1)}) custom-call(f32[3,8,40]{2,1,0:T(8,128)} %expand_hbm.1, s32[96]{0:T(128)} %rows_hbm.1, s32[96]{0:T(128)} %picks_hbm.1, bf16[40,4096]{1,0:T(8,128)(2,1)} %basis_hbm.1, bf16[3,96,128,128]{3,2,1,0:T(8,128)(2,1)} %tiles_hbm.1), custom_call_target="tpu_custom_call" | custom-call | tf_op jit(solution)/shard_map/pallas_call | solution.py:445
  26.3 0.7 %shard_map.77 = (f32[8,4096]{1,0:T(8,128)}, f32[8,40]{1,0:T(8,128)}, f32[8,8]{1,0:T(8,128)}) custom-call(f32[8,4096]{1,0:T(8,128)S(1)} %get-tuple-element.6.new_ref, f32[8,40]{1,0:T(8,128)S(1)} %get-tuple-element.7.coef_ref, f32[8,8]{1,0:T(8,128)S(1)} %get-tuple-element.8.factor_ref), custom_call_target="tpu_custom_call" | custom-call | tf_op jit(solution)/shard_map/pallas_call | solution.py:479

commit v5 on v3

--- a/solution.py
+++ b/solution.py
@@ -59,7 +59,7 @@
     tile_sem,
     ser_send,
     ser_recv,
-    fwd_recv,
+    rest_recv,
     seg_send,
     seg_recv,
     box_send,
@@ -85,8 +85,10 @@
     inverse_root = 1.0 / math.sqrt(entries)
     width = seg_in.shape[2]
 
-    load_basis = pltpu.make_async_copy(basis_hbm, basis, basis_sem)
-    load_basis.start()
+    parts = 4
+    for i in range(parts):
+        part = pl.ds(i * (length // parts), length // parts)
+        pltpu.make_async_copy(basis_hbm.at[:, part], basis.at[:, part], basis_sem).start()
     small = [
         pltpu.make_async_copy(src, dst, small_sem.at[i])
         for i, (src, dst) in enumerate(((expand_hbm, expand_ref), (rows_hbm, rows_ref), (picks_hbm, picks_ref)))
@@ -150,11 +152,11 @@
         return peer, {"col": peer}
 
     small[0].wait()
-    load_basis.wait()
+    pltpu.make_async_copy(basis_hbm, basis, basis_sem).wait()
     for m in range(kinds):
         for k in range(ncol):
             part = pl.ds(k * cap, cap)
-            pltpu.make_async_copy(tiles_hbm.at[m, part], tiles.at[m, part], tile_sem.at[m]).start()
+            pltpu.make_async_copy(tiles_hbm.at[m, part], tiles.at[m, part], tile_sem).start()
 
     def make(m):
         one = pieces(expand_ref[m])
@@ -162,18 +164,21 @@
             part = jnp.dot(one, basis[:, l * tile : (l + 1) * tile], preferred_element_type=F32)
             cols[m][r * region + l] = fold(part, bs).astype(BF16)
 
-    def series_copy(m, owner, peer, slot):
-        block = cols[m].at[pl.ds(owner * region, region)]
-        return remote(block, block, ser_send.at[m], ser_recv.at[m, slot], {"row": peer})
-
-    def pass_on(m, owner, h, peer, slot):
-        block = cols[m].at[pl.ds(owner * region + h * half, half)]
-        return remote(block, block, ser_send.at[m], fwd_recv.at[m, h, slot - 1], {"row": peer})
+    def block(m, owner, h):
+        return cols[m].at[pl.ds(owner * region + h * half, half)]
+
+    def first_half(m, owner, h, peer, slot):
+        part = block(m, owner, h)
+        return remote(part, part, ser_send.at[m], ser_recv.at[m, slot], {"row": peer})
+
+    def send_rest(m, owner, h, peer):
+        part = block(m, owner, h)
+        remote(part, part, ser_send.at[m], rest_recv.at[m], {"row": peer}).start()
 
     def spread(m):
-        series_copy(m, r, mate, 0).start()
+        first_half(m, r, 1, mate, 0).start()
         for j in range(1, outer):
-            series_copy(m, r, other(j), outer - j).start()
+            first_half(m, r, 0, other(j), outer - j).start()
 
     make(0)
 
@@ -186,6 +191,11 @@
     for m in range(1, kinds):
         make(m)
         spread(m)
+
+    for m in range(kinds):
+        send_rest(m, r, 0, mate)
+        for j in range(1, outer):
+            send_rest(m, r, 1, other(j))
 
     small[1].wait()
     small[2].wait()
@@ -208,18 +218,16 @@
     )
 
     def relay(m):
-        series_copy(m, mate, mate, 0).wait_recv()
+        first_half(m, mate, 1, mate, 0).wait_recv()
         for j in range(1, outer):
-            pass_on(m, mate, 1, other(j), outer - j).start()
+            send_rest(m, mate, 1, other(j))
         for j in range(1, outer):
-            series_copy(m, other(j), other(j), j).wait_recv()
-            pass_on(m, other(j), 0, mate, j).start()
+            first_half(m, other(j), 0, other(j), j).wait_recv()
+            send_rest(m, other(j), 0, mate)
 
     def relayed(m):
-        for j in range(1, outer):
-            far = other(j) + 1 - 2 * side
-            pass_on(m, far, 0, mate, j).wait_recv()
-            pass_on(m, far, 1, mate, j).wait_recv()
+        rest = cols[m].at[pl.ds(0, (3 * outer - 2) * half)]
+        pltpu.make_async_copy(rest, rest, rest_recv.at[m]).wait()
 
     relay(0)
     for i in range(rounds - 1):
@@ -239,8 +247,7 @@
     for m in range(kinds - 1):
         relayed(m)
 
-    for m in range(kinds):
-        pltpu.make_async_copy(tiles_hbm.at[m], tiles.at[m], tile_sem.at[m]).wait()
+    pltpu.make_async_copy(tiles_hbm, tiles, tile_sem).wait()
 
     def products(k, t, ms):
         out = []
@@ -257,21 +264,24 @@
     across = ncol // 2
     mine = lax.div(c, across)
 
+    upper = mine == 1
+
     def far_side(i):
-        return (1 - mine) * across + lax.rem(c + i, across)
+        return jnp.where(upper, i, ncol - 2 - 2 * lax.div(i, 2) + lax.rem(i, 2))
 
     def near_side(i):
-        return mine * across + lax.rem(c + i, across)
+        step = jnp.where(lax.rem(c, 2) == 1, i, lax.rem(i, across - 1) + 1)
+        return mine * across + lax.rem(c + step, across)
 
     early = held.shape[0]
     for i in range(early):
         for t in range(0, cap, 2):
-            held[i, t * bs : (t + 2) * bs] = products(far_side(i), t, range(kinds - 1))
+            held[i, t * bs : (t + 2) * bs] = products(far_side(jnp.int32(i)), t, range(kinds - 1))
 
     relayed(kinds - 1)
 
     for i in range(early):
-        k = far_side(i)
+        k = far_side(jnp.int32(i))
         for t in range(0, cap, 2):
             rows = slice(t * bs, (t + 2) * bs)
             outbox[k, rows] = (held[i, rows] + products(k, t, (kinds - 1,))).astype(BF16)
@@ -319,11 +329,11 @@
     me = r * ncol + c
     tail[me] = jnp.concatenate([raw[: bs // 2], raw[bs // 2 :]], axis=1)
 
-    for j in sorted(range(ncol), key=lambda j: -min(j, ncol - j)):
-        for i in reversed(range(nrow)):
-            if i or j:
-                where = {"row": lax.rem(r + i, nrow), "col": lax.rem(c + j, ncol)}
-                remote(tail.at[me], tail.at[me], tail_send, tail_recv, where).start()
+    columns = [far_side(jnp.int32(i)) for i in range(across)] + [near_side(jnp.int32(i)) for i in range(1, across)]
+    for k in columns + [c]:
+        for i in reversed(range(1 if k is c else 0, nrow)):
+            where = {"row": lax.rem(r + i, nrow), "col": k}
+            remote(tail.at[me], tail.at[me], tail_send, tail_recv, where).start()
 
     landed(corr_row, cr_recv)
     corr = jnp.sum(corr_row[...], axis=0) / entries
@@ -337,16 +347,12 @@
     before, after = 2 * bs, 64 - 2 * bs - krylov
     down, along = (lax.broadcasted_iota(jnp.int32, (64, bs), d) for d in (0, 1))
     gather = ((down == along) | (down == along + bs)).astype(F32) / entries
-    mix = jnp.concatenate(
-        [
-            jnp.pad(both * inverse_root, ((before, after), (0, 0))),
-            gather,
-            jnp.zeros((64, 64 + before - krylov - bs), F32),
-            jnp.pad(kern, ((before, after), (0, after))),
-        ],
-        axis=1,
+    narrow = jnp.concatenate(
+        [jnp.pad(both * inverse_root, ((before, after), (0, 0))), gather, jnp.zeros((64, 128 - krylov - bs), F32)], axis=1
     )
-    mix = jnp.concatenate([mix, jnp.zeros((64, 128), F32)], axis=0)
+    kern = jnp.pad(kern, ((before, after), (before, after)))
+    mix = jnp.concatenate([kern, kern, narrow], axis=1)
+    mix = jnp.concatenate([mix, jnp.zeros((64, 256), F32)], axis=0)
     coarse = mix.astype(BF16).astype(F32)
     mix = jnp.concatenate([coarse, mix - coarse], axis=1).astype(BF16)
     right = lax.broadcasted_iota(jnp.int32, (bs, 128), 1) >= 64
@@ -357,12 +363,11 @@
     total = jnp.sum(tail[...], axis=0)
     turned = jnp.concatenate([total[:, 64:], total[:, :64]], axis=1)
     total = jnp.where(right == below, jnp.concatenate([total, total], axis=0), jnp.concatenate([turned, turned], axis=0))
-    total = pieces(total)
-    made = fold(jnp.dot(total, mix, preferred_element_type=F32), bs)
-    made = made[:, :128] + made[:, 128:]
-    taken = pieces(jnp.where(right, made, 0.0))
-    taken = fold(lax.dot_general(taken, total, NT, preferred_element_type=F32), bs)
-    gram = made[:, krylov : krylov + bs] - (taken[:, :bs] + taken[:, bs:])
+    lead = total.astype(BF16).astype(F32)
+    made = fold(jnp.dot(pieces(total), mix, preferred_element_type=F32), bs)
+    taken, made = made[:, :128] + made[:, 256:384], made[:, 128:256] + made[:, 384:]
+    total = jnp.where(right, total - lead, lead).astype(BF16)
+    gram = made[:, krylov : krylov + bs] - fold(lax.dot_general(pieces(taken), total, NT, preferred_element_type=F32), bs)
     coefficients = made[:, :krylov]
     coef_ref[...] = coefficients
 
@@ -448,13 +453,13 @@
             pltpu.VMEM((nrow, band, lanes), F32),
             pltpu.VMEM((nrow * ncol, bs // 2, 128), F32),
             pltpu.VMEM((region * bs, tpd * bs), BF16),
-            pltpu.VMEM((2, cap * bs, tile), F32),
+            pltpu.VMEM((1, cap * bs, tile), F32),
             dma((3,)),
             dma,
-            dma((kinds,)),
+            dma,
             dma((kinds,)),
             dma((kinds, nrow // 2)),
-            dma((kinds, 2, nrow // 2 - 1)),
+            dma((kinds,)),
         ]
         + [dma] * 10
         + [pltpu.SemaphoreType.REGULAR((max(ncol // 2 - 2, 1),))] * 2,

time: 28.8 us -> 26.2 us (0.910)
  Pallas kernels: 27.9 us -> 25.4 us
    pallas_call x1, Pallas kernels: 27.2 us -> 24.7 us  [shards(): pl.pallas_call(functools.partial(kernel, nrow, ncol), out_shape=shapes, i...]
where the time goes in v5:
time: 26.2 us; the launch traced here: 26 us
  Pallas kernels  25.4 us (97%)
  between operations  0.64 us (2%)
    pallas_call x1, Pallas kernels, shards(): pl.pallas_call(functools.partial(kernel, nrow, ncol), out_shape=shapes, i...  24.7 us
    pallas_call x1, Pallas kernels, shards(): pl.pallas_call(leave, out_shape=shapes, in_specs=[vmem] * 3, out_specs=(h...  0.69 us

profile of v5, /device:TPU:0, one launch (start us, length us, event | category | flops | bytes accessed | tf_op | source)
XLA Modules:
  0.0 26.0 jit_solution(902414199764030252)
XLA Ops:
  0.6 24.7 %shard_map.76 = (f32[8,4096]{1,0:T(8,128)S(1)}, f32[8,40]{1,0:T(8,128)S(1)}, f32[8,8]{1,0:T(8,128)S(1)}) custom-call(f32[3,8,40]{2,1,0:T(8,128)} %expand_hbm.1, s32[96]{0:T(128)} %rows_hbm.1, s32[96]{0:T(128)} %picks_hbm.1, bf16[40,4096]{1,0:T(8,128)(2,1)} %basis_hbm.1, bf16[3,96,128,128]{3,2,1,0:T(8,128)(2,1)} %tiles_hbm.1), custom_call_target="tpu_custom_call" | custom-call | tf_op jit(solution)/shard_map/pallas_call | solution.py:436
  25.3 0.7 %shard_map.77 = (f32[8,4096]{1,0:T(8,128)}, f32[8,40]{1,0:T(8,128)}, f32[8,8]{1,0:T(8,128)}) custom-call(f32[8,4096]{1,0:T(8,128)S(1)} %get-tuple-element.6.new_ref, f32[8,40]{1,0:T(8,128)S(1)} %get-tuple-element.7.coef_ref, f32[8,8]{1,0:T(8,128)S(1)} %get-tuple-element.8.factor_ref), custom_call_target="tpu_custom_call" | custom-call | tf_op jit(solution)/shard_map/pallas_call | solution.py:470

commit v6 on v5

--- a/solution.py
+++ b/solution.py
@@ -273,37 +273,38 @@
         step = jnp.where(lax.rem(c, 2) == 1, i, lax.rem(i, across - 1) + 1)
         return mine * across + lax.rem(c + step, across)
 
+    far = [far_side(jnp.int32(i)) for i in range(across)]
+    near = [near_side(jnp.int32(i)) for i in range(1, across)]
     early = held.shape[0]
     for i in range(early):
         for t in range(0, cap, 2):
-            held[i, t * bs : (t + 2) * bs] = products(far_side(jnp.int32(i)), t, range(kinds - 1))
+            held[i, t * bs : (t + 2) * bs] = products(far[i], t, range(kinds - 1))
 
     relayed(kinds - 1)
-
-    for i in range(early):
-        k = far_side(jnp.int32(i))
-        for t in range(0, cap, 2):
-            rows = slice(t * bs, (t + 2) * bs)
-            outbox[k, rows] = (held[i, rows] + products(k, t, (kinds - 1,))).astype(BF16)
-        box_copy(k).start()
 
     def whole(k, dst):
         for t in range(0, cap, 2):
             dst[k, t * bs : (t + 2) * bs] = products(k, t, range(kinds)).astype(BF16)
 
-    def send_far(i, carry):
-        whole(far_side(i), outbox)
-        box_copy(far_side(i)).start()
+    for i in range(early):
+        for t in range(0, cap, 2):
+            rows = slice(t * bs, (t + 2) * bs)
+            outbox[far[i], rows] = (held[i, rows] + products(far[i], t, (kinds - 1,))).astype(BF16)
+        box_copy(far[i]).start()
+
+    def pick(s):
+        others = across - 2
+        k = jnp.where(s < others, near_side(s + 1), near_side(jnp.int32(across - 1)))
+        at = s - others + early
+        return jnp.where((s >= others) & (at < across), far_side(at), k)
+
+    def send(s, carry):
+        k = pick(s)
+        whole(k, outbox)
+        box_copy(k).start()
         return carry
 
-    def send_near(i, carry):
-        whole(near_side(i), outbox)
-        box_copy(near_side(i)).start()
-        return carry
-
-    lax.fori_loop(early, across, send_far, 0)
-    lax.fori_loop(1, across, send_near, 0)
-
+    lax.fori_loop(0, 2 * across - 1 - early, send, 0)
     whole(c, inbox)
 
     landed(corr_col, cc_recv)
@@ -329,11 +330,19 @@
     me = r * ncol + c
     tail[me] = jnp.concatenate([raw[: bs // 2], raw[bs // 2 :]], axis=1)
 
-    columns = [far_side(jnp.int32(i)) for i in range(across)] + [near_side(jnp.int32(i)) for i in range(1, across)]
-    for k in columns + [c]:
-        for i in reversed(range(1 if k is c else 0, nrow)):
-            where = {"row": lax.rem(r + i, nrow), "col": k}
-            remote(tail.at[me], tail.at[me], tail_send, tail_recv, where).start()
+    def give(row, col):
+        remote(tail.at[me], tail.at[me], tail_send, tail_recv, {"row": row, "col": col}).start()
+
+    columns = far + near
+    for pair in range(0, across, 2):
+        for i in range(nrow):
+            for k in columns[pair : pair + 2]:
+                give(i, k)
+    for k in columns[across:]:
+        for i in range(nrow):
+            give(i, k)
+    for i in range(1, nrow):
+        give(lax.rem(r + i, nrow), c)
 
     landed(corr_row, cr_recv)
     corr = jnp.sum(corr_row[...], axis=0) / entries
@@ -347,33 +356,43 @@
     before, after = 2 * bs, 64 - 2 * bs - krylov
     down, along = (lax.broadcasted_iota(jnp.int32, (64, bs), d) for d in (0, 1))
     gather = ((down == along) | (down == along + bs)).astype(F32) / entries
-    narrow = jnp.concatenate(
-        [jnp.pad(both * inverse_root, ((before, after), (0, 0))), gather, jnp.zeros((64, 128 - krylov - bs), F32)], axis=1
+    mix = jnp.concatenate(
+        [
+            jnp.pad(both * inverse_root, ((before, after), (0, 0))),
+            gather,
+            jnp.zeros((64, 64 + before - krylov - bs), F32),
+            jnp.pad(kern, ((before, after), (0, after))),
+        ],
+        axis=1,
     )
-    kern = jnp.pad(kern, ((before, after), (before, after)))
-    mix = jnp.concatenate([kern, kern, narrow], axis=1)
-    mix = jnp.concatenate([mix, jnp.zeros((64, 256), F32)], axis=0)
+    mix = jnp.concatenate([mix, jnp.zeros((64, 128), F32)], axis=0)
     coarse = mix.astype(BF16).astype(F32)
     mix = jnp.concatenate([coarse, mix - coarse], axis=1).astype(BF16)
-    right = lax.broadcasted_iota(jnp.int32, (bs, 128), 1) >= 64
-    below = lax.broadcasted_iota(jnp.int32, (bs, 128), 0) >= bs // 2
+    sub = lax.broadcasted_iota(jnp.int32, (bs, 128), 0)
+    lane = lax.broadcasted_iota(jnp.int32, (bs, 128), 1)
+    right, below = lane >= 64, sub >= bs // 2
 
     landed(tail, tail_recv)
 
-    total = jnp.sum(tail[...], axis=0)
+    sums = [tail[i] for i in range(nrow * ncol)]
+    while len(sums) > 1:
+        sums = [sum(sums[i : i + 2]) for i in range(0, len(sums), 2)]
+    total = sums[0]
     turned = jnp.concatenate([total[:, 64:], total[:, :64]], axis=1)
     total = jnp.where(right == below, jnp.concatenate([total, total], axis=0), jnp.concatenate([turned, turned], axis=0))
-    lead = total.astype(BF16).astype(F32)
     made = fold(jnp.dot(pieces(total), mix, preferred_element_type=F32), bs)
-    taken, made = made[:, :128] + made[:, 256:384], made[:, 128:256] + made[:, 384:]
-    total = jnp.where(right, total - lead, lead).astype(BF16)
-    gram = made[:, krylov : krylov + bs] - fold(lax.dot_general(pieces(taken), total, NT, preferred_element_type=F32), bs)
+    made = made[:, :128] + made[:, 128:]
+    columns = [jnp.zeros((bs, 128), F32)] * bs
+    for d in range(bs):
+        energy = jnp.where(lane == krylov + lax.rem(sub + d, bs), made, 0.0)
+        turned = total if d == 0 else pltpu.roll(total, bs - d, 0)
+        gram = jnp.sum(jnp.where(right, -made * turned, energy), axis=1, keepdims=True)
+        for j in range(bs):
+            if (j - d) % bs >= j:
+                columns[j] = jnp.where(sub == (j - d) % bs, gram, columns[j])
     coefficients = made[:, :krylov]
     coef_ref[...] = coefficients
 
-    sub = lax.broadcasted_iota(jnp.int32, (bs, tile), 0)
-    lane = lax.broadcasted_iota(jnp.int32, (bs, tile), 1)
-    columns = [jnp.broadcast_to(gram[:, j : j + 1], (bs, tile)) for j in range(bs)]
     factor = jnp.zeros((bs, tile), F32)
     inverse = jnp.zeros((bs, tile), F32)
     for j in range(bs):
@@ -453,7 +472,7 @@
             pltpu.VMEM((nrow, band, lanes), F32),
             pltpu.VMEM((nrow * ncol, bs // 2, 128), F32),
             pltpu.VMEM((region * bs, tpd * bs), BF16),
-            pltpu.VMEM((1, cap * bs, tile), F32),
+            pltpu.VMEM((2, cap * bs, tile), F32),
             dma((3,)),
             dma,
             dma,

time: 26.2 us -> 25.3 us (0.966)
  Pallas kernels: 25.4 us -> 24.5 us
    pallas_call x1, Pallas kernels: 24.7 us -> 23.8 us  [shards(): pl.pallas_call(functools.partial(kernel, nrow, ncol), out_shape=shapes, i...]
where the time goes in v6:
time: 25.3 us; the launch traced here: 25.2 us
  Pallas kernels  24.5 us (97%)
  between operations  0.64 us (3%)
    pallas_call x1, Pallas kernels, shards(): pl.pallas_call(functools.partial(kernel, nrow, ncol), out_shape=shapes, i...  23.8 us
    pallas_call x1, Pallas kernels, shards(): pl.pallas_call(leave, out_shape=shapes, in_specs=[vmem] * 3, out_specs=(h...  0.69 us

profile of v6, /device:TPU:0, one launch (start us, length us, event | category | flops | bytes accessed | tf_op | source)
XLA Modules:
  0.0 25.2 jit_solution(4900783981875178889)
XLA Ops:
  0.6 23.8 %shard_map.76 = (f32[8,4096]{1,0:T(8,128)S(1)}, f32[8,40]{1,0:T(8,128)S(1)}, f32[8,8]{1,0:T(8,128)S(1)}) custom-call(f32[3,8,40]{2,1,0:T(8,128)} %expand_hbm.1, s32[96]{0:T(128)} %rows_hbm.1, s32[96]{0:T(128)} %picks_hbm.1, bf16[40,4096]{1,0:T(8,128)(2,1)} %basis_hbm.1, bf16[3,96,128,128]{3,2,1,0:T(8,128)(2,1)} %tiles_hbm.1), custom_call_target="tpu_custom_call" | custom-call | tf_op jit(solution)/shard_map/pallas_call | solution.py:455
  24.5 0.7 %shard_map.77 = (f32[8,4096]{1,0:T(8,128)}, f32[8,40]{1,0:T(8,128)}, f32[8,8]{1,0:T(8,128)}) custom-call(f32[8,4096]{1,0:T(8,128)S(1)} %get-tuple-element.6.new_ref, f32[8,40]{1,0:T(8,128)S(1)} %get-tuple-element.7.coef_ref, f32[8,8]{1,0:T(8,128)S(1)} %get-tuple-element.8.factor_ref), custom_call_target="tpu_custom_call" | custom-call | tf_op jit(solution)/shard_map/pallas_call | solution.py:489

commit v7 on v6

--- a/solution.py
+++ b/solution.py
@@ -153,11 +153,6 @@
 
     small[0].wait()
     pltpu.make_async_copy(basis_hbm, basis, basis_sem).wait()
-    for m in range(kinds):
-        for k in range(ncol):
-            part = pl.ds(k * cap, cap)
-            pltpu.make_async_copy(tiles_hbm.at[m, part], tiles.at[m, part], tile_sem).start()
-
     def make(m):
         one = pieces(expand_ref[m])
         for l in range(region):
@@ -196,6 +191,11 @@
         send_rest(m, r, 0, mate)
         for j in range(1, outer):
             send_rest(m, r, 1, other(j))
+
+    for m in range(kinds):
+        for k in range(ncol):
+            part = pl.ds(k * cap, cap)
+            pltpu.make_async_copy(tiles_hbm.at[m, part], tiles.at[m, part], tile_sem).start()
 
     small[1].wait()
     small[2].wait()
@@ -236,14 +236,14 @@
     relay(1)
     if rounds > 0:
         hear(rounds - 1)
+    for m in range(2, kinds):
+        relay(m)
     for j in range(1, ncol):
         peer, where = col_at(j)
         remote(seg_out.at[peer], seg_in.at[c], seg_send, seg_recv, where).start()
     for j in range(1, ncol):
         peer, where = col_at(j)
         remote(corr_col.at[c], corr_col.at[c], cc_send, cc_recv, where).start()
-    for m in range(2, kinds):
-        relay(m)
     for m in range(kinds - 1):
         relayed(m)
 

time: 25.3 us -> 25.3 us (level)
  no operation moved by 1% of the time
where the time goes in v7:
time: 25.3 us; the launch traced here: 25.2 us
  Pallas kernels  24.5 us (97%)
  between operations  0.64 us (3%)
    pallas_call x1, Pallas kernels, shards(): pl.pallas_call(functools.partial(kernel, nrow, ncol), out_shape=shapes, i...  23.8 us
    pallas_call x1, Pallas kernels, shards(): pl.pallas_call(leave, out_shape=shapes, in_specs=[vmem] * 3, out_specs=(h...  0.69 us

profile of v7, /device:TPU:0, one launch (start us, length us, event | category | flops | bytes accessed | tf_op | source)
XLA Modules:
  0.0 25.2 jit_solution(15712497298075218515)
XLA Ops:
  0.6 23.8 %shard_map.76 = (f32[8,4096]{1,0:T(8,128)S(1)}, f32[8,40]{1,0:T(8,128)S(1)}, f32[8,8]{1,0:T(8,128)S(1)}) custom-call(f32[3,8,40]{2,1,0:T(8,128)} %expand_hbm.1, s32[96]{0:T(128)} %rows_hbm.1, s32[96]{0:T(128)} %picks_hbm.1, bf16[40,4096]{1,0:T(8,128)(2,1)} %basis_hbm.1, bf16[3,96,128,128]{3,2,1,0:T(8,128)(2,1)} %tiles_hbm.1), custom_call_target="tpu_custom_call" | custom-call | tf_op jit(solution)/shard_map/pallas_call | solution.py:455
  24.5 0.7 %shard_map.77 = (f32[8,4096]{1,0:T(8,128)}, f32[8,40]{1,0:T(8,128)}, f32[8,8]{1,0:T(8,128)}) custom-call(f32[8,4096]{1,0:T(8,128)S(1)} %get-tuple-element.6.new_ref, f32[8,40]{1,0:T(8,128)S(1)} %get-tuple-element.7.coef_ref, f32[8,8]{1,0:T(8,128)S(1)} %get-tuple-element.8.factor_ref), custom_call_target="tpu_custom_call" | custom-call | tf_op jit(solution)/shard_map/pallas_call | solution.py:489

commit v8 on v7

--- a/solution.py
+++ b/solution.py
@@ -294,9 +294,10 @@
 
     def pick(s):
         others = across - 2
-        k = jnp.where(s < others, near_side(s + 1), near_side(jnp.int32(across - 1)))
-        at = s - others + early
-        return jnp.where((s >= others) & (at < across), far_side(at), k)
+        first = s == 0
+        at = jnp.where(first, early, s - others + early)
+        k = near_side(jnp.where(s <= others, jnp.maximum(s, 1), across - 1))
+        return jnp.where(first | ((s > others) & (at < across)), far_side(at), k)
 
     def send(s, carry):
         k = pick(s)

time: 25.3 us -> 25.3 us (level)
  no operation moved by 1% of the time
where the time goes in v8:
time: 25.3 us; the launch traced here: 25.1 us
  Pallas kernels  24.5 us (97%)
  between operations  0.64 us (3%)
    pallas_call x1, Pallas kernels, shards(): pl.pallas_call(functools.partial(kernel, nrow, ncol), out_shape=shapes, i...  23.8 us
    pallas_call x1, Pallas kernels, shards(): pl.pallas_call(leave, out_shape=shapes, in_specs=[vmem] * 3, out_specs=(h...  0.69 us

profile of v8, /device:TPU:0, one launch (start us, length us, event | category | flops | bytes accessed | tf_op | source)
XLA Modules:
  0.0 25.1 jit_solution(16195838413054920834)
XLA Ops:
  0.6 23.8 %shard_map.76 = (f32[8,4096]{1,0:T(8,128)S(1)}, f32[8,40]{1,0:T(8,128)S(1)}, f32[8,8]{1,0:T(8,128)S(1)}) custom-call(f32[3,8,40]{2,1,0:T(8,128)} %expand_hbm.1, s32[96]{0:T(128)} %rows_hbm.1, s32[96]{0:T(128)} %picks_hbm.1, bf16[40,4096]{1,0:T(8,128)(2,1)} %basis_hbm.1, bf16[3,96,128,128]{3,2,1,0:T(8,128)(2,1)} %tiles_hbm.1), custom_call_target="tpu_custom_call" | custom-call | tf_op jit(solution)/shard_map/pallas_call | solution.py:456
  24.5 0.7 %shard_map.77 = (f32[8,4096]{1,0:T(8,128)}, f32[8,40]{1,0:T(8,128)}, f32[8,8]{1,0:T(8,128)}) custom-call(f32[8,4096]{1,0:T(8,128)S(1)} %get-tuple-element.6.new_ref, f32[8,40]{1,0:T(8,128)S(1)} %get-tuple-element.7.coef_ref, f32[8,8]{1,0:T(8,128)S(1)} %get-tuple-element.8.factor_ref), custom_call_target="tpu_custom_call" | custom-call | tf_op jit(solution)/shard_map/pallas_call | solution.py:490
